TPU v7x, 32 devices: a whole 2x2x4 slice. The times are simulated.
32 devices in a mesh: dp: 2 (over x), tp: 4 (over z), pp: 4 (over y, core).
Axes of the slice: x: 2, y: 2, z: 4, core: 2. Of those that a mesh axis runs over, the one named last changes fastest.
Arguments:
- stage_buf: bfloat16 [4, 16, 512, 2560], P('pp', 'dp', 'tp'), parts along dimension 1
- new_mb: bfloat16 [16, 512, 2560], P('dp', 'tp'), parts along dimension 0
- positions: int32 [512], replicated
- ln_attn: float32 [4, 2, 2560], P('pp')
- ln_mlp: float32 [4, 2, 2560], P('pp')
- w_qkv: bfloat16 [4, 32, 3, 80, 2560], P('pp', 'tp')
- w_out: bfloat16 [4, 2560, 2560], P('pp', 'tp')
- w_up: bfloat16 [4, 2560, 10240], P('pp', None, 'tp')
- w_down: bfloat16 [4, 10240, 2560], P('pp', 'tp')
Outputs:
- output 1: bfloat16 [16, 512, 2560], P('dp', 'tp', 'pp'), parts along dimension 0
- output 2: bfloat16 [16, 512, 2560], P('dp', 'tp', 'pp'), parts along dimension 0
- output 3: bfloat16 [4, 16, 512, 2560], P('pp', 'dp', 'tp'), parts along dimension 1
There are 2 independent parts. A program takes and returns all parts, laid end to end along the dimension named above; an argument that names none is the same for every part.
All inputs are finite; a program needn't handle non-finite values.
Results may differ from a plain program's by a relative error of at most 0.0179774.
Values are sent between devices in bfloat16 or wider.
A program may use at most 1 GiB of HBM per device.

v0:
```python
import jax
import jax.numpy as jnp
from jax import lax
from jax.sharding import PartitionSpec as P

LN_EPS = 1e-5
ROPE_BASE = 10000.0


def rope_tables(positions, head_dim):
    inv_freq = 1.0 / (ROPE_BASE ** (jnp.arange(0, head_dim, 2).astype(jnp.float32) / head_dim))
    angles = positions.astype(jnp.float32)[:, None] * inv_freq[None, :]
    return jnp.cos(angles), jnp.sin(angles)


def layer_norm(x_in, ln_params):
    x_wide = x_in.astype(jnp.float32)
    centered = x_wide - jnp.mean(x_wide, axis=-1, keepdims=True)
    variance = jnp.mean(jnp.square(centered), axis=-1, keepdims=True)
    return (centered * lax.rsqrt(variance + LN_EPS) * ln_params[0] + ln_params[1]).astype(jnp.bfloat16)


def rotate_half(x_in, cos_tab, sin_tab):
    half_dim = x_in.shape[-1] // 2
    x_wide = x_in.astype(jnp.float32)
    first_half = x_wide[..., :half_dim]
    second_half = x_wide[..., half_dim:]
    return jnp.concatenate([first_half * cos_tab - second_half * sin_tab, second_half * cos_tab + first_half * sin_tab], axis=-1).astype(jnp.bfloat16)


def attention_heads(a_norm, w_qkv, cos_tab, sin_tab):
    groups = w_qkv.shape[1] - 2
    head_dim = w_qkv.shape[2]
    seq_len = a_norm.shape[1]
    qkv_proj = jnp.einsum("nsd,kjhd->nskjh", a_norm, w_qkv, preferred_element_type=jnp.float32).astype(jnp.bfloat16)
    queries = rotate_half(qkv_proj[:, :, :, :groups], cos_tab[:, None, None], sin_tab[:, None, None])
    key_rot = rotate_half(qkv_proj[:, :, :, groups], cos_tab[:, None], sin_tab[:, None])
    values = qkv_proj[:, :, :, groups + 1]
    scores = jnp.einsum("nskgh,ntkh->nkgst", queries, key_rot, preferred_element_type=jnp.float32) * head_dim ** -0.5
    causal = jnp.arange(seq_len)[:, None] >= jnp.arange(seq_len)[None, :]
    attn_probs = jax.nn.softmax(jnp.where(causal, scores, -1e30), axis=-1).astype(jnp.bfloat16)
    return jnp.einsum("nkgst,ntkh->nskgh", attn_probs, values, preferred_element_type=jnp.float32).astype(jnp.bfloat16)


def local_layer(x_loc, ln_attn, ln_mlp, w_qkv, w_out, w_up, w_down, cos_tab, sin_tab):
    x_full = lax.all_gather(x_loc, "tp", axis=1, tiled=True)
    attn_heads = attention_heads(layer_norm(x_full, ln_attn), w_qkv, cos_tab, sin_tab)
    kv_local, groups, head_dim = attn_heads.shape[2], attn_heads.shape[3], attn_heads.shape[4]
    attn_part = jnp.einsum("nskgh,kghd->nsd", attn_heads, w_out.reshape(kv_local, groups, head_dim, w_out.shape[-1]), preferred_element_type=jnp.float32)
    hidden = jax.nn.gelu(jnp.einsum("nsd,df->nsf", layer_norm(x_full, ln_mlp), w_up, preferred_element_type=jnp.float32), approximate=False).astype(jnp.bfloat16)
    mlp_part = jnp.einsum("nsf,fd->nsd", hidden, w_down, preferred_element_type=jnp.float32)
    part_sum = (attn_part + mlp_part).astype(jnp.bfloat16)
    reduced = lax.psum_scatter(part_sum, "tp", scatter_dimension=1, tiled=True)
    return (x_loc.astype(jnp.float32) + reduced.astype(jnp.float32)).astype(jnp.bfloat16)


def solution(mesh):
    stages = mesh.shape["pp"]
    shift_pairs = [(src_stage, src_stage + 1) for src_stage in range(stages - 1)]
    act_spec = P("dp", "tp", None)
    buf_spec = P("pp", "dp", "tp", None)
    emit_spec = P("dp", "tp", "pp")
    stack_spec = P("pp", None, None)

    def stage_body(stage_buf, new_mb, positions, ln_attn, ln_mlp, w_qkv, w_out, w_up, w_down):
        stage_idx = lax.axis_index("pp")
        cos_tab, sin_tab = rope_tables(positions, w_qkv.shape[3])

        def layer_here(x_loc):
            return local_layer(x_loc, ln_attn[0], ln_mlp[0], w_qkv[0], w_out[0], w_up[0], w_down[0], cos_tab, sin_tab)

        def emit_last(y_loc):
            masked = jnp.where(stage_idx == stages - 1, y_loc, jnp.zeros_like(y_loc))
            return lax.psum_scatter(masked, "pp", scatter_dimension=2, tiled=True)

        y_one = layer_here(stage_buf[0])
        emit_one = emit_last(y_one)
        shifted = lax.ppermute(y_one, "pp", shift_pairs)
        buf_one = jnp.where(stage_idx == 0, new_mb, shifted)
        y_two = layer_here(buf_one)
        emit_two = emit_last(y_two)
        final_buf = lax.ppermute(y_two, "pp", shift_pairs)
        return emit_one, emit_two, final_buf[None]

    return jax.shard_map(stage_body, mesh=mesh, in_specs=(buf_spec, act_spec, P(None), stack_spec, stack_spec, P("pp", "tp", None, None, None), P("pp", "tp", None), P("pp", None, "tp"), P("pp", "tp", None)), out_specs=(emit_spec, emit_spec, buf_spec), check_vma=False)
```

profile of v0, /device:TPU:6, one launch (start us, length us, event | category | flops | bytes accessed | tf_op | source)
XLA Modules:
  0.0 2506.5 jit_solution(4586098098085575964)
XLA Ops:
  8.0 0.9 convert_element_type.124
  8.8 0.9 slice_reduce_fusion.3
  9.7 1.5 slice_reduce_fusion.1
  11.2 0.8 iota_compare_fusion
  12.4 355.1 %all-gather.6.cloned.1.call-done = bf16[1,8,512,2560]{3,2,1,0:T(8,128)(2,1)} async-done(((bf16[1,8,128,2560]{3,2,1,0:T(8,128)(2,1)}), bf16[1,8,512,2560]{3,2,1,0:T(8,128)(2,1)}) %all-gather.6.cloned.1.call-update) | async-done | bytes 20971536 | tf_op jit(solution)/shard_map/all_gather | solution.py:46
  367.4 11.0 convert_reduce_fusion
  378.5 11.9 fusion.22
  390.5 46.5 %fusion.144 = bf16[8,512,8,3,80]{1,4,3,2,0:T(8,128)(2,1)} fusion(bf16[1,8,512,2560]{3,2,1,0:T(8,128)(2,1)S(1)} %bitcast.250, f32[2560]{0:T(1024)S(1)} %get-tuple-element.10, f32[2560]{0:T(1024)S(1)} %get-tuple-element.9, f32[8,512]{1,0:T(8,128)S(1)} %add_rsqrt_fusion.1, f32[8,512]{1,0:T(8,128)S(1)} %broadcast_multiply_fusion.1, ...), kind=kOutput, calls=%fused_computation.177 | convolution fusion | flops 40336097280 | bytes 46583808 | tf_op jit(solution)/shard_map/nsd,kjhd->nskjh/dot_general | solution.py:35
  437.0 12.1 slice_convert_fusion.1
  449.1 5.5 fusion.193
  454.5 5.6 fusion.192
  460.1 17.7 subtract_convert_fusion.2
  477.9 28.5 %fusion.2 = (f32[8,8,512]{2,1,0:T(8,128)}, f32[8,8,512,512]{3,2,1,0:T(8,128)}) fusion(pred[512,512]{0,1:T(8,128)(4,1)} %iota_compare_fusion, bf16[8,512,8,40]{1,3,2,0:T(8,128)(2,1)} %fusion.193, bf16[8,512,8,40]{1,3,2,0:T(8,128)(2,1)} %fusion.192, bf16[8,512,8,40]{1,3,2,0:T(8,128)(2,1)} %get-tuple-element.25, bf16[8,512,8,40]{1,3,2,0:T(8,128)(2,1)} %get-tuple-element.24), kind=kOutput, calls=%fused_computation.14 | convolution fusion | flops 2755624960 | bytes 77987840 | tf_op jit(solution)/shard_map/nskgh,ntkh->nkgst/dot_general | solution.py:39
  506.4 22.4 fusion
  528.8 45.9 %fusion.175 = f32[8,512,2560,1]{2,1,3,0:T(8,128)} fusion(bf16[8,80,2560,1]{2,1,0,3:T(8,128)(2,1)S(1)} %bitcast.247, f32[8,8,512,512]{3,2,1,0:T(8,128)} %get-tuple-element.29, f32[8,8,512]{2,1,0:T(8,128)} %fusion, f32[8,8,512]{2,1,0:T(8,128)} %get-tuple-element.28, pred[512,512]{0,1:T(8,128)(4,1)S(1)} %copy-done.6, bf16[8,512,8,3,80]{1,4,3,2,0:T(8,128)(2,1)} %fusion.144), kind=kOutput, calls=%fused_computation.210 | convolution fusion | flops 16192634880 | bytes 118095872 | tf_op jit(solution)/shard_map/nskgh,kghd->nsd/dot_general | solution.py:49
  574.7 77.8 %fusion.142 = (u8[512,2560]{1,0:T(8,128)(4,1)}, u8[512,2560]{1,0:T(8,128)(4,1)}, f32[8,512,2560]{2,1,0:T(8,128)}) fusion(bf16[1,2560,2560]{2,1,0:T(8,128)(2,1)} %param.16, bf16[1,8,512,2560]{3,2,1,0:T(8,128)(2,1)} %all-gather.6.cloned.1.call-done, f32[2560]{0:T(1024)} %get-tuple-element.8, f32[2560]{0:T(1024)} %get-tuple-element.7, ...), kind=kOutput, calls=%fused_computation.175 | convolution fusion | flops 53883699200 | bytes 78696448 | tf_op jit(solution)/shard_map/nsd,df->nsf/dot_general | solution.py:50
  652.5 149.6 %fusion.30 = bf16[8,512,2560]{2,1,0:T(8,128)(2,1)} fusion(f32[8,512,2560,1]{2,1,3,0:T(8,128)} %fusion.175, f32[8,512,2560]{2,1,0:T(8,128)} %get-tuple-element.30, bf16[1,2560,2560]{2,1,0:T(8,128)(2,1)} %param.17, u8[512,2560]{1,0:T(8,128)(4,1)} %get-tuple-element.6, u8[512,2560]{1,0:T(8,128)(4,1)} %get-tuple-element.5), kind=kOutput, calls=%fused_computation.53 | convolution fusion | flops 54442065920 | bytes 120586240 | tf_op jit(solution)/shard_map/nsf,fd->nsd/dot_general | solution.py:51
  802.2 345.9 %reduce-scatter.9.cloned.1.call-done = bf16[8,128,2560]{2,1,0:T(8,128)(2,1)} async-done(((bf16[8,512,2560]{2,1,0:T(8,128)(2,1)}), bf16[8,128,2560]{2,1,0:T(8,128)(2,1)}) %reduce-scatter.9.cloned.1.call-update) | async-done | bytes 5242896 | tf_op jit(solution)/shard_map/reduce_scatter | solution.py:53
  1148.1 10.2 broadcast_select_fusion.2
  1158.3 1.9 collective-permute-start
  1160.2 59.4 %collective-permute-done = bf16[8,128,2560]{2,1,0:T(8,128)(2,1)} collective-permute-done((bf16[8,128,2560]{2,1,0:T(8,128)(2,1)}, bf16[8,128,2560]{2,1,0:T(8,128)(2,1)}, u32[]{:S(2)}, u32[]{:S(2)}) %collective-permute-start) | collective-permute-done | bytes 5242912 | tf_op jit(solution)/shard_map/ppermute | solution.py:78
  1219.7 5.3 broadcast_select_fusion
  1225.1 358.0 %all-gather.4.cloned.1.call-done = bf16[8,512,2560]{2,1,0:T(8,128)(2,1)} async-done(((bf16[8,128,2560]{2,1,0:T(8,128)(2,1)}), bf16[8,512,2560]{2,1,0:T(8,128)(2,1)}) %all-gather.4.cloned.1.call-update) | async-done | bytes 20971536 | tf_op jit(solution)/shard_map/all_gather | solution.py:46
  1583.1 8.4 convert_reduce_fusion.1
  1591.6 10.2 fusion.12
  1602.5 52.5 %fusion.148 = bf16[8,512,8,3,80]{1,4,2,0,3:T(8,128)(2,1)} fusion(bf16[8,512,2560]{2,1,0:T(8,128)(2,1)} %all-gather.4.cloned.1.call-done, f32[8,512]{1,0:T(8,128)S(1)} %add_rsqrt_fusion, f32[8,512]{1,0:T(8,128)S(1)} %broadcast_multiply_fusion, f32[2560]{0:T(1024)S(1)} %copy-done.17, f32[2560]{0:T(1024)S(1)} %copy-done.15, ...), kind=kOutput, calls=%fused_computation.179 | convolution fusion | flops 40336097280 | bytes 46583808 | tf_op jit(solution)/shard_map/nsd,kjhd->nskjh/dot_general | solution.py:35
  1655.0 14.3 slice_convert_fusion
  1669.2 6.4 fusion.190
  1675.7 6.5 subtract_convert_fusion.1
  1682.2 28.9 %fusion.3 = (f32[8,8,512]{2,1,0:T(8,128)}, f32[8,8,512,512]{3,2,1,0:T(8,128)}) fusion(pred[512,512]{0,1:T(8,128)(4,1)} %iota_compare_fusion, bf16[8,512,8,40]{1,3,2,0:T(8,128)(2,1)} %get-tuple-element.21, bf16[8,512,8,40]{1,3,2,0:T(8,128)(2,1)} %get-tuple-element.20, bf16[8,512,8,40]{1,3,2,0:T(8,128)(2,1)} %get-tuple-element.23, ...), kind=kOutput, calls=%fused_computation.15 | convolution fusion | flops 2755624960 | bytes 77987840 | tf_op jit(solution)/shard_map/nskgh,ntkh->nkgst/dot_general | solution.py:39
  1711.1 22.4 fusion.1
  1733.5 45.9 %fusion.173 = f32[8,512,2560,1]{2,1,3,0:T(8,128)} fusion(bf16[8,80,2560,1]{2,1,0,3:T(8,128)(2,1)S(1)} %bitcast.248, f32[8,8,512,512]{3,2,1,0:T(8,128)} %get-tuple-element.32, f32[8,8,512]{2,1,0:T(8,128)} %fusion.1, f32[8,8,512]{2,1,0:T(8,128)} %get-tuple-element.31, pred[512,512]{0,1:T(8,128)(4,1)S(1)} %copy-done.7, bf16[8,512,8,3,80]{1,4,2,0,3:T(8,128)(2,1)} %fusion.148), kind=kOutput, calls=%fused_computation.208 | convolution fusion | flops 16192634880 | bytes 118095872 | tf_op jit(solution)/shard_map/nskgh,kghd->nsd/dot_general | solution.py:49
  1779.4 76.7 %fusion.143 = (u8[512,2560]{1,0:T(8,128)(4,1)S(1)}, u8[512,2560]{1,0:T(8,128)(4,1)S(1)}, f32[8,512,2560]{2,1,0:T(8,128)}) fusion(bf16[1,2560,2560]{2,1,0:T(8,128)(2,1)} %param.16, bf16[8,512,2560]{2,1,0:T(8,128)(2,1)} %all-gather.4.cloned.1.call-done, f32[8,512]{1,0:T(8,128)} %copy-done.12, f32[8,512]{1,0:T(8,128)S(1)} %copy-done.9, ...), kind=kOutput, calls=%fused_computation.176 | convolution fusion | flops 53883699200 | bytes 78696448 | tf_op jit(solution)/shard_map/nsd,df->nsf/dot_general | solution.py:50
  1856.0 149.3 %fusion.29 = bf16[8,512,2560]{2,1,0:T(8,128)(2,1)} fusion(f32[8,512,2560,1]{2,1,3,0:T(8,128)} %fusion.173, f32[8,512,2560]{2,1,0:T(8,128)} %get-tuple-element.33, bf16[1,2560,2560]{2,1,0:T(8,128)(2,1)} %param.17, u8[512,2560]{1,0:T(8,128)(4,1)S(1)} %get-tuple-element.4, u8[512,2560]{1,0:T(8,128)(4,1)S(1)} %get-tuple-element.3), kind=kOutput, calls=%fused_computation.51 | convolution fusion | flops 54442065920 | bytes 120586240 | tf_op jit(solution)/shard_map/nsf,fd->nsd/dot_general | solution.py:51
  2005.4 8.4 copy.36
  2013.8 6.4 copy.52
  2020.3 331.0 %reduce-scatter.11.cloned.1.call-done = bf16[8,128,2560]{2,1,0:T(8,128)(2,1)} async-done(((bf16[8,512,2560]{2,1,0:T(8,128)(2,1)}), bf16[8,128,2560]{2,1,0:T(8,128)(2,1)}) %reduce-scatter.11.cloned.1.call-update) | async-done | bytes 5242896 | tf_op jit(solution)/shard_map/reduce_scatter | solution.py:53
  2351.3 10.2 broadcast_select_fusion.1
  2361.5 8.7 copy.38
  2370.2 6.5 copy.51
  2376.7 1.9 collective-permute-start.1
  2378.7 38.8 %reduce-scatter.13.cloned.1.call-done = bf16[640,1024]{1,0:T(8,128)(2,1)} async-done(((bf16[2560,1024]{1,0:T(8,128)(2,1)}), bf16[640,1024]{1,0:T(8,128)(2,1)}) %reduce-scatter.13.cloned.1.call-update) | async-done | bytes 1310736
  2417.4 2.7 copy.42
  2420.2 2.8 copy.37
  2422.9 65.8 %collective-permute-done.1 = bf16[8,128,2560]{2,1,0:T(8,128)(2,1)} collective-permute-done((bf16[8,128,2560]{2,1,0:T(8,128)(2,1)}, bf16[8,128,2560]{2,1,0:T(8,128)(2,1)}, u32[]{:S(2)}, u32[]{:S(2)}) %collective-permute-start.1) | collective-permute-done | bytes 5242912 | tf_op jit(solution)/shard_map/ppermute | solution.py:82
  2488.8 2.7 copy.44
  2491.5 2.8 copy.39
  2494.3 5.2 copy.54
  (66 shorter events, 2.1 us)
Async XLA Ops:
  7.2 521.7 %copy-start = (bf16[1,640,2560]{2,1,0:T(8,128)(2,1)S(1)}, bf16[1,640,2560]{2,1,0:T(8,128)(2,1)}, u32[]{:S(2)}) copy-start(bf16[1,640,2560]{2,1,0:T(8,128)(2,1)} %param.15) | copy-start | bytes 9830404
  7.2 360.2 %all-gather.6.cloned.1.call-start = ((), (), s32[]{:S(2)}) async-start(), calls=%async_computation.7 | async-start | bytes 26214400 | tf_op jit(solution)/shard_map/all_gather | solution.py:46
  7.9 1140.2 %reduce-scatter.9.cloned.1.call-start = ((), (), s32[]{:S(2)}) async-start(), calls=%async_computation.4 | async-start | bytes 26214400 | tf_op jit(solution)/shard_map/reduce_scatter | solution.py:53
  9.7 427.2 %copy-start.14 = (f32[2560]{0:T(1024)}, f32[2560]{0:T(1024)S(1)}, u32[]{:S(2)}) copy-start(f32[2560]{0:T(1024)S(1)} %get-tuple-element.9) | copy-start | bytes 30724
  9.7 427.2 %copy-start.16 = (f32[2560]{0:T(1024)}, f32[2560]{0:T(1024)S(1)}, u32[]{:S(2)}) copy-start(f32[2560]{0:T(1024)S(1)} %get-tuple-element.10) | copy-start | bytes 30724
  12.3 447.8 %copy-start.2 = (f32[512,40]{0,1:T(8,128)}, f32[512,40]{0,1:T(8,128)S(1)}, u32[]{:S(2)}) copy-start(f32[512,40]{0,1:T(8,128)S(1)} %get-tuple-element.26) | copy-start | bytes 245764
  12.3 447.8 %copy-start.4 = (f32[512,40]{0,1:T(8,128)}, f32[512,40]{0,1:T(8,128)S(1)}, u32[]{:S(2)}) copy-start(f32[512,40]{0,1:T(8,128)S(1)} %get-tuple-element.27) | copy-start | bytes 245764
  367.4 23.0 slice-start
  367.4 23.0 slice-start.1
  367.4 23.0 slice-start.2
  378.5 58.5 %copy-start.10 = (f32[8,512]{1,0:T(8,128)}, f32[8,512]{1,0:T(8,128)S(1)}, u32[]{:S(2)}) copy-start(f32[8,512]{1,0:T(8,128)S(1)} %broadcast_multiply_fusion.1) | copy-start | bytes 49156
  378.5 12.0 slice-start.3
  378.5 12.0 slice-start.4
  390.4 46.6 %copy-start.13 = (f32[8,512]{1,0:T(8,128)}, f32[8,512]{1,0:T(8,128)S(1)}, u32[]{:S(2)}) copy-start(f32[8,512]{1,0:T(8,128)S(1)} %add_rsqrt_fusion.1) | copy-start | bytes 49156
  477.9 28.6 %copy-start.6 = (pred[512,512]{0,1:T(8,128)(4,1)S(1)}, pred[512,512]{0,1:T(8,128)(4,1)}, u32[]{:S(2)}) copy-start(pred[512,512]{0,1:T(8,128)(4,1)} %iota_compare_fusion) | copy-start | bytes 786436
  528.8 45.9 %copy-start.11 = (f32[8,512]{1,0:T(8,128)S(1)}, f32[8,512]{1,0:T(8,128)}, u32[]{:S(2)}) copy-start(f32[8,512]{1,0:T(8,128)} %copy-done.10) | copy-start | bytes 49156
  802.1 781.0 %all-gather.4.cloned.1.call-start = ((), (), s32[]{:S(2)}) async-start(), calls=%async_computation.5 | async-start | bytes 26214400 | tf_op jit(solution)/shard_map/all_gather | solution.py:46
  802.2 800.3 %copy-start.15 = (f32[2560]{0:T(1024)S(1)}, f32[2560]{0:T(1024)}, u32[]{:S(2)}) copy-start(f32[2560]{0:T(1024)} %copy-done.14) | copy-start | bytes 30724
  802.2 800.3 %copy-start.17 = (f32[2560]{0:T(1024)S(1)}, f32[2560]{0:T(1024)}, u32[]{:S(2)}) copy-start(f32[2560]{0:T(1024)} %copy-done.16) | copy-start | bytes 30724
  1158.3 61.4 %collective-permute-start = (bf16[8,128,2560]{2,1,0:T(8,128)(2,1)}, bf16[8,128,2560]{2,1,0:T(8,128)(2,1)}, u32[]{:S(2)}, u32[]{:S(2)}) collective-permute-start(bf16[8,128,2560]{2,1,0:T(8,128)(2,1)} %get-tuple-element.14), channel_id=1, source_target_pairs={{0,1},{1,2},{2,3},{4,5},{5,6},{6,7},{8,9},{9,10},{10,11},{12,13},{... | collective-permute-start | bytes 15728648 | tf_op jit(solution)/shard_map/ppermute | solution.py:78
  1225.0 1126.3 %reduce-scatter.11.cloned.1.call-start = ((), (), s32[]{:S(2)}) async-start(), calls=%async_computation.6 | async-start | bytes 26214400 | tf_op jit(solution)/shard_map/reduce_scatter | solution.py:53
  1591.6 10.3 copy-start.8
  1601.9 0.6 copy-start.12
  1602.5 66.8 %copy-start.3 = (f32[512,40]{0,1:T(8,128)S(1)}, f32[512,40]{0,1:T(8,128)}, u32[]{:S(2)}) copy-start(f32[512,40]{0,1:T(8,128)} %copy-done.2) | copy-start | bytes 245764
  1602.5 66.8 %copy-start.5 = (f32[512,40]{0,1:T(8,128)S(1)}, f32[512,40]{0,1:T(8,128)}, u32[]{:S(2)}) copy-start(f32[512,40]{0,1:T(8,128)} %copy-done.4) | copy-start | bytes 245764
  1682.2 28.9 %copy-start.7 = (pred[512,512]{0,1:T(8,128)(4,1)S(1)}, pred[512,512]{0,1:T(8,128)(4,1)}, u32[]{:S(2)}) copy-start(pred[512,512]{0,1:T(8,128)(4,1)} %iota_compare_fusion) | copy-start | bytes 786436
  1733.5 45.9 %copy-start.9 = (f32[8,512]{1,0:T(8,128)S(1)}, f32[8,512]{1,0:T(8,128)}, u32[]{:S(2)}) copy-start(f32[8,512]{1,0:T(8,128)} %copy-done.8) | copy-start | bytes 49156
  2005.4 412.1 %reduce-scatter.13.cloned.1.call-start = ((), (), s32[]{:S(2)}) async-start(), calls=%async_computation.8 | async-start | bytes 6553600
  2013.8 485.6 %copy-start.1 = (bf16[1,640,2560]{2,1,0:T(8,128)(2,1)S(1)}, bf16[1,640,2560]{2,1,0:T(8,128)(2,1)}, u32[]{:S(2)}) copy-start(bf16[1,640,2560]{2,1,0:T(8,128)(2,1)} %param.15) | copy-start | bytes 9830404
  2020.2 468.5 %reduce-scatter.15.cloned.1.call-start = ((), (), s32[]{:S(2)}) async-start(), calls=%async_computation.9 | async-start | bytes 6553600
  2376.7 112.0 %collective-permute-start.1 = (bf16[8,128,2560]{2,1,0:T(8,128)(2,1)}, bf16[8,128,2560]{2,1,0:T(8,128)(2,1)}, u32[]{:S(2)}, u32[]{:S(2)}) collective-permute-start(bf16[8,128,2560]{2,1,0:T(8,128)(2,1)} %get-tuple-element.12), channel_id=1, source_target_pairs={{0,1},{1,2},{2,3},{4,5},{5,6},{6,7},{8,9},{9,10},{10,11},{12,13},{... | collective-permute-start | bytes 15728648 | tf_op jit(solution)/shard_map/ppermute | solution.py:82
Sparse Core Ops, SparseCore 0:
  9.6 357.8 all-gather.5
  802.3 345.7 reduce-scatter.8
  1225.1 357.9 all-gather.3
  2005.5 345.8 reduce-scatter.10
  2354.3 63.0 reduce-scatter.12
  2419.8 65.3 reduce-scatter.14
where the time goes:
time: 2520 us; the launch traced here: 2510 us
  waiting for transfers between devices  1550 us (62%)
  matrix products  702 us (28%)
  other arithmetic  182 us (7%)
  local copies, waits for them, and re-layouts  49.2 us (2%)
    all_gather x2, waiting for transfers between devices, local_layer(): x_full = lax.all_gather(x_loc, 'tp', axis=1, tiled=True)  713 us
    reduce_scatter x2, waiting for transfers between devices, local_layer(): reduced = lax.psum_scatter(part_sum, 'tp', scatter_dimension=1, tiled=True)  677 us
    dot_general x2, matrix products, local_layer(): jnp.einsum('nsf,fd->nsd', hidden, w_down, preferred_element_type=jnp.floa...  299 us
    dot_general x2, matrix products, local_layer(): jnp.einsum('nsd,df->nsf', layer_norm(x_full, ln_mlp), w_up, preferred_ele...  154 us
    dot_general x2, matrix products, attention_heads(): jnp.einsum('nsd,kjhd->nskjh', a_norm, w_qkv, preferred_element_type=jnp.f...  99 us
    dot_general x2, matrix products, local_layer(): jnp.einsum('nskgh,kghd->nsd', attn_heads, w_out.reshape(kv_local, groups,...  91.8 us
    ppermute x1, waiting for transfers between devices, stage_body(): final_buf = lax.ppermute(y_two, 'pp', shift_pairs)  65.8 us
    ppermute x1, waiting for transfers between devices, stage_body(): shifted = lax.ppermute(y_one, 'pp', shift_pairs)  59.4 us
  transfers between devices with their start and end apart: 8, of which 7 were waited for; matrix products, arithmetic and copies ran while one was open for 2% of the time, Pallas kernels for 0%

commit v1 on v0

v1 whole, which is shorter than its diff:
```python
import functools

import jax
import jax.numpy as jnp
from jax import lax
from jax.experimental import pallas as pl
from jax.experimental.pallas import tpu as pltpu
from jax.sharding import PartitionSpec as P


LN_EPS = 1e-5
ROPE_BASE = 10000.0
CHUNKS = 4


def rope_tables(positions, head_dim):
    inv_freq = 1.0 / (ROPE_BASE ** (jnp.arange(0, head_dim, 2).astype(jnp.float32) / head_dim))
    angles = positions.astype(jnp.float32)[:, None] * inv_freq[None, :]
    return jnp.cos(angles), jnp.sin(angles)


def rotate_half(x_in, cos_tab, sin_tab):
    half_dim = x_in.shape[-1] // 2
    x_wide = x_in.astype(jnp.float32)
    first_half = x_wide[..., :half_dim]
    second_half = x_wide[..., half_dim:]
    return jnp.concatenate([first_half * cos_tab - second_half * sin_tab, second_half * cos_tab + first_half * sin_tab], axis=-1).astype(jnp.bfloat16)


def norm_kernel(n, rank_ref, *refs):
    own_ref, from_left, from_right = refs[0], refs[1:n], refs[n : 2 * n - 1]
    ln_ref, a_ref, m_ref = refs[2 * n - 1 :]
    k = pl.program_id(1)
    rank = rank_ref[0]

    def write(x_ref):
        x_wide = x_ref[0].astype(jnp.float32)
        centered = x_wide - jnp.mean(x_wide, axis=-1, keepdims=True)
        variance = jnp.mean(jnp.square(centered), axis=-1, keepdims=True)
        normed = centered * lax.rsqrt(variance + LN_EPS)
        a_ref[0] = (normed * ln_ref[0:1, :] + ln_ref[1:2, :]).astype(jnp.bfloat16)
        m_ref[0] = (normed * ln_ref[2:3, :] + ln_ref[3:4, :]).astype(jnp.bfloat16)

    pl.when(k == 0)(lambda: write(own_ref))
    for step in range(1, n):
        pl.when(jnp.logical_and(k == step, rank >= step))(lambda: write(from_left[step - 1]))
        pl.when(jnp.logical_and(k == step, rank < step))(lambda: write(from_right[n - step - 1]))


def both_norms(rank, own, from_left, from_right, ln_rows):
    n = len(from_left) + 1
    seqs, rows, width = own.shape
    piece = pl.BlockSpec((1, rows, width), lambda b, k, rank: (b, 0, 0))
    out = pl.BlockSpec((1, rows, width), lambda b, k, rank: (b, k, 0))
    shape = jax.ShapeDtypeStruct((seqs, n * rows, width), jnp.bfloat16)
    return pl.pallas_call(
        functools.partial(norm_kernel, n),
        grid_spec=pltpu.PrefetchScalarGridSpec(
            num_scalar_prefetch=1,
            grid=(seqs, n),
            in_specs=[piece] * (2 * n - 1) + [pl.BlockSpec((4, width), lambda b, k, rank: (0, 0))],
            out_specs=[out, out],
        ),
        out_shape=[shape, shape],
        cost_estimate=pl.CostEstimate(flops=40 * seqs * n * rows * width * 100, bytes_accessed=2 * (4 * n - 1) * seqs * rows * width, transcendentals=0),
        name="both_norms",
    )(rank, own, *from_left, *from_right, ln_rows)


def down_kernel(n, rank_ref, o_ref, g_ref, w_out_ref, w_down_ref, *p_refs):
    seqs, rows = p_refs[0].shape[0], p_refs[0].shape[1]
    part = jnp.dot(g_ref[...], w_down_ref[...], preferred_element_type=jnp.float32)
    part += jnp.dot(o_ref[...], w_out_ref[...], preferred_element_type=jnp.float32)
    part = part.astype(jnp.bfloat16)
    for b in range(seqs):
        for k in range(n):
            start = (b * n + k) * rows
            p_refs[k][b] = part[start : start + rows]

    def first_send(k):
        for b in range(seqs):
            p_refs[n][b] = p_refs[k][b]

    pl.when(rank_ref[0] == 0)(lambda: first_send(1))
    pl.when(rank_ref[0] != 0)(lambda: first_send(n - 1))


def out_and_down(rank, n, seqs, heads_out, hidden, w_out, w_down, block=512):
    tokens, width = hidden.shape[0], w_down.shape[1]
    rows = tokens // (n * seqs)
    return pl.pallas_call(
        functools.partial(down_kernel, n),
        grid_spec=pltpu.PrefetchScalarGridSpec(
            num_scalar_prefetch=1,
            grid=(width // block,),
            in_specs=[
                pl.BlockSpec((tokens, heads_out.shape[1]), lambda j, rank: (0, 0)),
                pl.BlockSpec((tokens, hidden.shape[1]), lambda j, rank: (0, 0)),
                pl.BlockSpec((w_out.shape[0], block), lambda j, rank: (0, j)),
                pl.BlockSpec((w_down.shape[0], block), lambda j, rank: (0, j)),
            ],
            out_specs=[pl.BlockSpec((seqs, rows, block), lambda j, rank: (0, 0, j))] * (n + 1),
        ),
        out_shape=[jax.ShapeDtypeStruct((seqs, rows, width), jnp.bfloat16)] * (n + 1),
        compiler_params=pltpu.CompilerParams(vmem_limit_bytes=56 * 1024 * 1024),
        cost_estimate=pl.CostEstimate(flops=2 * tokens * width * (w_out.shape[0] + w_down.shape[0]), bytes_accessed=2 * (w_out.size + w_down.size + hidden.size + heads_out.size + tokens * width), transcendentals=0),
        name="out_and_down",
    )(rank, heads_out, hidden, w_out, w_down)


def line_gather(x_loc, n):
    from_left, from_right = [x_loc], [x_loc]
    for step in range(1, n):
        from_left.append(lax.ppermute(from_left[-1], "tp", [(z, z + 1) for z in range(step - 1, n - 1)]))
        from_right.append(lax.ppermute(from_right[-1], "tp", [(z, z - 1) for z in range(1, n - step + 1)]))
    return from_left[1:], from_right[1:]


def line_scatter(parts, first_send):
    inward = lax.ppermute(first_send, "tp", [(0, 1), (3, 2)])
    middle = parts[2] + inward
    rightward = lax.ppermute(middle, "tp", [(0, 1), (1, 2)])
    leftward = lax.ppermute(middle, "tp", [(3, 2), (2, 1)])
    send_right, send_left = parts[3] + rightward, parts[1] + leftward
    rightward = lax.ppermute(send_right, "tp", [(0, 1), (1, 2), (2, 3)])
    leftward = lax.ppermute(send_left, "tp", [(3, 2), (2, 1), (1, 0)])
    return parts[0].astype(jnp.float32) + rightward.astype(jnp.float32) + leftward.astype(jnp.float32)


def attention_heads(a_norm, w_qkv, cos_tab, sin_tab, causal):
    groups = w_qkv.shape[1] - 2
    head_dim = w_qkv.shape[2]
    qkv_proj = jnp.einsum("nsd,kjhd->nskjh", a_norm, w_qkv, preferred_element_type=jnp.float32).astype(jnp.bfloat16)
    queries = rotate_half(qkv_proj[:, :, :, :groups], cos_tab[:, None, None], sin_tab[:, None, None])
    key_rot = rotate_half(qkv_proj[:, :, :, groups], cos_tab[:, None], sin_tab[:, None])
    values = qkv_proj[:, :, :, groups + 1]
    scores = jnp.einsum("nskgh,ntkh->nkgst", queries, key_rot, preferred_element_type=jnp.float32) * head_dim ** -0.5
    attn_probs = jax.nn.softmax(jnp.where(causal, scores, -1e30), axis=-1).astype(jnp.bfloat16)
    return jnp.einsum("nkgst,ntkh->nskgh", attn_probs, values, preferred_element_type=jnp.float32).astype(jnp.bfloat16)


def solution(mesh):
    stages = mesh.shape["pp"]
    n = mesh.shape["tp"]
    shift_pairs = [(src_stage, src_stage + 1) for src_stage in range(stages - 1)]
    act_spec = P("dp", "tp", None)
    buf_spec = P("pp", "dp", "tp", None)
    emit_spec = P("dp", "tp", "pp")
    stack_spec = P("pp", None, None)

    def stage_body(stage_buf, new_mb, positions, ln_attn, ln_mlp, w_qkv, w_out, w_up, w_down):
        stage_idx = lax.axis_index("pp")
        rank = lax.axis_index("tp")
        seqs = stage_buf.shape[1] // CHUNKS
        rows, width = stage_buf.shape[2], stage_buf.shape[3]
        order = (rank + n - jnp.arange(n)) % n
        token_idx = (order[:, None] * rows + jnp.arange(rows)[None, :]).reshape(-1)
        cos_tab, sin_tab = rope_tables(positions[token_idx], w_qkv.shape[3])
        causal = token_idx[:, None] >= token_idx[None, :]
        ln_rows = jnp.concatenate([ln_attn[0], ln_mlp[0]], axis=0)
        rank_arr = rank.astype(jnp.int32)[None]

        def layer_here(x_loc):
            from_left, from_right = line_gather(x_loc, n)
            a_norm, m_norm = both_norms(rank_arr, x_loc, from_left, from_right, ln_rows)
            a_norm, cos_here, sin_here, causal_here = lax.optimization_barrier((a_norm, cos_tab, sin_tab, causal))
            heads_out = attention_heads(a_norm, w_qkv[0], cos_here, sin_here, causal_here)
            hidden = jnp.dot(m_norm.reshape(-1, width), w_up[0], preferred_element_type=jnp.float32)
            hidden = jax.nn.gelu(hidden, approximate=False).astype(jnp.bfloat16)
            *parts, first_send = out_and_down(rank_arr, n, seqs, heads_out.reshape(seqs * n * rows, -1), hidden, w_out[0], w_down[0])
            x_late, parts = lax.optimization_barrier((x_loc, parts))
            reduced = line_scatter(parts, first_send)
            return (x_late.astype(jnp.float32) + reduced).astype(jnp.bfloat16)

        def emit_last(y_list):
            block = width // stages

            def columns(dst):
                return jnp.concatenate([y[..., dst * block : (dst + 1) * block] for y in y_list])

            mine = jnp.where(stage_idx == stages - 1, columns(stages - 1), jnp.zeros((), y_list[0].dtype))
            for dst in range(stages - 1):
                mine = mine + lax.ppermute(columns(dst), "pp", [(stages - 1, dst)])
            return mine

        def shift(y_loc):
            return lax.ppermute(y_loc, "pp", shift_pairs)

        first, second, bufs, final_buf = [], [], [], []
        for c in range(CHUNKS):
            first.append(layer_here(stage_buf[0, c * seqs : (c + 1) * seqs]))
            shifted, fresh = lax.optimization_barrier((shift(first[c]), new_mb[c * seqs : (c + 1) * seqs]))
            bufs.append(jnp.where(stage_idx == 0, fresh, shifted))
        emit_one = emit_last(first)
        for c in range(CHUNKS):
            second.append(layer_here(bufs[c]))
            final_buf.append(shift(second[c]))
        emit_two = jnp.concatenate([emit_last(second[:-1]), emit_last(second[-1:])])
        return emit_one, emit_two, jnp.concatenate(final_buf)[None]

    return jax.shard_map(stage_body, mesh=mesh, in_specs=(buf_spec, act_spec, P(None), stack_spec, stack_spec, P("pp", "tp", None, None, None), P("pp", "tp", None), P("pp", None, "tp"), P("pp", "tp", None)), out_specs=(emit_spec, emit_spec, buf_spec), check_vma=False)
```

time: 2520 us -> 2170 us (0.86)
  waiting for transfers between devices: 1550 us -> 782 us
  Pallas kernels: 0 us -> 296 us
  starting transfers between devices: 4.07 us -> 270 us
  matrix products: 702 us -> 570 us
    all_gather x2 -> x0, waiting for transfers between devices: 713 us -> none  [local_layer(): x_full = lax.all_gather(x_loc, 'tp', axis=1, tiled=True)]
    reduce_scatter x2 -> x0, waiting for transfers between devices: 677 us -> none  [local_layer(): reduced = lax.psum_scatter(part_sum, 'tp', scatter_dimension=1, tiled=True)]
    ppermute x2 -> x105, waiting for transfers between devices: 125 us -> 782 us  [the longest x24 314 us: line_gather(): lax.ppermute(from_right[-1], 'tp', [(z, z - 1) for z in range(1, n - step...]
    pallas_call x0 -> x16, Pallas kernels: none -> 296 us  [the longest x8 190 us: out_and_down(): pl.pallas_call(functools.partial(down_kernel, n), grid_spec=pltpu.Prefetc...]
    ppermute x2 -> x105, starting transfers between devices: 3.83 us -> 270 us  [the longest x8 68.9 us: line_scatter(): rightward = lax.ppermute(send_right, 'tp', [(0, 1), (1, 2), (2, 3)])]
    dot_general x6 -> x16, matrix products: 545 us -> 392 us  [the longest x8 318 us: layer_here(): jnp.dot(m_norm.reshape(-1, width), w_up[0], preferred_element_type=jnp.fl...]
    unnamed x55 -> x276, local copies, waits for them, and re-layouts: 46.9 us -> 3.63 us
    reduce_sum x4 -> x0, other arithmetic: 41.6 us -> none  [the longest x2 22.1 us: layer_norm(): variance = jnp.mean(jnp.square(centered), axis=-1, keepdims=True)]
  transfers between devices with their start and end apart: 8 -> 105, of which waited for: 7 -> 48; matrix products, arithmetic and copies ran while one was open for 2% -> 28% of each run, Pallas kernels for 0% -> 10%
where the time goes in v1:
time: 2170 us; the launch traced here: 2160 us
  waiting for transfers between devices  782 us (36%)
  matrix products  570 us (26%)
  Pallas kernels  296 us (14%)
  starting transfers between devices  270 us (12%)
  other arithmetic  179 us (8%)
  local copies, waits for them, and re-layouts  61.5 us (3%)
    dot_general x8, matrix products, layer_here(): jnp.dot(m_norm.reshape(-1, width), w_up[0], preferred_element_type=jnp.fl...  318 us
    ppermute x24, waiting for transfers between devices, line_gather(): lax.ppermute(from_right[-1], 'tp', [(z, z - 1) for z in range(1, n - step...  314 us
    pallas_call x8, Pallas kernels, out_and_down(): pl.pallas_call(functools.partial(down_kernel, n), grid_spec=pltpu.Prefetc...  190 us
    ppermute x8, waiting for transfers between devices, line_scatter(): rightward = lax.ppermute(send_right, 'tp', [(0, 1), (1, 2), (2, 3)])  134 us
    ppermute x8, waiting for transfers between devices, line_scatter(): rightward = lax.ppermute(middle, 'tp', [(0, 1), (1, 2)])  132 us
    dot_general x8, matrix products, attention_heads(): jnp.einsum('nsd,kjhd->nskjh', a_norm, w_qkv, preferred_element_type=jnp.f...  117 us
    ppermute x24, waiting for transfers between devices, line_gather(): lax.ppermute(from_left[-1], 'tp', [(z, z + 1) for z in range(step - 1, n...  115 us
    pallas_call x8, Pallas kernels, both_norms(): pl.pallas_call(functools.partial(norm_kernel, n), grid_spec=pltpu.Prefetc...  106 us
  transfers between devices with their start and end apart: 105, of which 48 were waited for; matrix products, arithmetic and copies ran while one was open for 28% of the time, Pallas kernels for 10%

profile of v1, /device:TPU:6, one launch (start us, length us, event | category | flops | bytes accessed | tf_op | source)
XLA Modules:
  0.0 2161.1 jit_solution(5844330067865978454)
XLA Ops:
  21.2 15.3 collective-permute-done.33.refs_1_
  44.4 20.1 collective-permute-done.22.refs_1_
  70.8 21.8 %collective-permute-done.11.refs_1_ = bf16[2,128,2560]{2,1,0:T(8,128)(2,1)} collective-permute-done((bf16[2,128,2560]{2,1,0:T(8,128)(2,1)S(1)}, bf16[2,128,2560]{2,1,0:T(8,128)(2,1)}, u32[]{:S(2)}, u32[]{:S(2)}) %collective-permute-start.11) | collective-permute-done | bytes 1310752 | tf_op jit(solution)/shard_map/ppermute | solution.py:114
  98.8 20.8 collective-permute-done.refs_1_
  128.7 24.7 %collective-permute-done.37.refs_5_ = bf16[2,128,2560]{2,1,0:T(8,128)(2,1)} collective-permute-done((bf16[2,128,2560]{2,1,0:T(8,128)(2,1)S(1)}, bf16[2,128,2560]{2,1,0:T(8,128)(2,1)}, u32[]{:S(2)}, u32[]{:S(2)}) %collective-permute-start.37) | collective-permute-done | bytes 1310752 | tf_op jit(solution)/shard_map/ppermute | solution.py:115
  160.2 21.2 collective-permute-done.26.refs_5_
  186.2 23.4 %collective-permute-done.38.refs_6_ = bf16[2,128,2560]{2,1,0:T(8,128)(2,1)} collective-permute-done((bf16[2,128,2560]{2,1,0:T(8,128)(2,1)}, bf16[2,128,2560]{2,1,0:T(8,128)(2,1)}, u32[]{:S(2)}, u32[]{:S(2)}) %collective-permute-start.38) | collective-permute-done | bytes 1310752 | tf_op jit(solution)/shard_map/ppermute | solution.py:115
  240.6 25.1 %collective-permute-done.4.refs_5_ = bf16[2,128,2560]{2,1,0:T(8,128)(2,1)} collective-permute-done((bf16[2,128,2560]{2,1,0:T(8,128)(2,1)}, bf16[2,128,2560]{2,1,0:T(8,128)(2,1)}, u32[]{:S(2)}, u32[]{:S(2)}) %collective-permute-start.4) | collective-permute-done | bytes 1310752 | tf_op jit(solution)/shard_map/ppermute | solution.py:115
  268.9 24.9 %collective-permute-done.27.refs_6_ = bf16[2,128,2560]{2,1,0:T(8,128)(2,1)} collective-permute-done((bf16[2,128,2560]{2,1,0:T(8,128)(2,1)}, bf16[2,128,2560]{2,1,0:T(8,128)(2,1)}, u32[]{:S(2)}, u32[]{:S(2)}) %collective-permute-start.27) | collective-permute-done | bytes 1310752 | tf_op jit(solution)/shard_map/ppermute | solution.py:115
  444.2 39.7 %fusion.43.g_ref = bf16[1024,2560]{1,0:T(8,128)(2,1)} fusion(bf16[1024,2560]{1,0:T(8,128)(2,1)} %bitcast.711, bf16[1,2560,2560]{2,1,0:T(8,128)(2,1)} %param.16), kind=kOutput, calls=%fused_computation.76 | convolution fusion | flops 13592166400 | bytes 23592960 | tf_op jit(solution)/shard_map/dot_general | solution.py:168
  483.9 23.8 %out_and_down.11 = (bf16[2,128,2560]{2,1,0:T(8,128)(2,1)}, bf16[2,128,2560]{2,1,0:T(8,128)(2,1)}, bf16[2,128,2560]{2,1,0:T(8,128)(2,1)}, bf16[2,128,2560]{2,1,0:T(8,128)(2,1)}, bf16[2,128,2560]{2,1,0:T(8,128)(2,1)}) custom-call(s32[1]{0:T(128)} %bitcast.1.rank_ref, bf16[1024,640]{1,0:T(8,128)(2,1)} %reshape.524.o_ref, bf16[1024,2560]{1,0:T(8,128)(2,1)} %fusion.43.g_ref, ...), custom_call_target="tpu_custom_call" | custom-call | flops 16777216000 | bytes 28180480 | tf_op jit(solution)/shard_map/out_and_down/pallas_call | solution.py:91
  542.7 40.0 %fusion.40.g_ref = bf16[1024,2560]{1,0:T(8,128)(2,1)} fusion(bf16[1024,2560]{1,0:T(8,128)(2,1)} %bitcast.712, bf16[1,2560,2560]{2,1,0:T(8,128)(2,1)} %param.16), kind=kOutput, calls=%fused_computation.73 | convolution fusion | flops 13592166400 | bytes 23592960 | tf_op jit(solution)/shard_map/dot_general | solution.py:168
  582.7 23.8 %out_and_down.10 = (bf16[2,128,2560]{2,1,0:T(8,128)(2,1)}, bf16[2,128,2560]{2,1,0:T(8,128)(2,1)}, bf16[2,128,2560]{2,1,0:T(8,128)(2,1)}, bf16[2,128,2560]{2,1,0:T(8,128)(2,1)}, bf16[2,128,2560]{2,1,0:T(8,128)(2,1)}) custom-call(s32[1]{0:T(128)} %bitcast.1.rank_ref, bf16[1024,640]{1,0:T(8,128)(2,1)} %reshape.523.o_ref, bf16[1024,2560]{1,0:T(8,128)(2,1)} %fusion.40.g_ref, ...), custom_call_target="tpu_custom_call" | custom-call | flops 16777216000 | bytes 28180480 | tf_op jit(solution)/shard_map/out_and_down/pallas_call | solution.py:91
  641.3 39.7 %fusion.37.g_ref = bf16[1024,2560]{1,0:T(8,128)(2,1)} fusion(bf16[1024,2560]{1,0:T(8,128)(2,1)} %bitcast.710, bf16[1,2560,2560]{2,1,0:T(8,128)(2,1)} %param.16), kind=kOutput, calls=%fused_computation.70 | convolution fusion | flops 13592166400 | bytes 23592960 | tf_op jit(solution)/shard_map/dot_general | solution.py:168
  681.0 23.8 %out_and_down.9 = (bf16[2,128,2560]{2,1,0:T(8,128)(2,1)}, bf16[2,128,2560]{2,1,0:T(8,128)(2,1)}, bf16[2,128,2560]{2,1,0:T(8,128)(2,1)}, bf16[2,128,2560]{2,1,0:T(8,128)(2,1)}, bf16[2,128,2560]{2,1,0:T(8,128)(2,1)}) custom-call(s32[1]{0:T(128)} %bitcast.1.rank_ref, bf16[1024,640]{1,0:T(8,128)(2,1)} %reshape.522.o_ref, bf16[1024,2560]{1,0:T(8,128)(2,1)} %fusion.37.g_ref, ...), custom_call_target="tpu_custom_call" | custom-call | flops 16777216000 | bytes 28180480 | tf_op jit(solution)/shard_map/out_and_down/pallas_call | solution.py:91
  737.5 39.7 %fusion.34.g_ref = bf16[1024,2560]{1,0:T(8,128)(2,1)} fusion(bf16[1024,2560]{1,0:T(8,128)(2,1)} %bitcast.708, bf16[1,2560,2560]{2,1,0:T(8,128)(2,1)} %param.16), kind=kOutput, calls=%fused_computation.67 | convolution fusion | flops 13592166400 | bytes 23592960 | tf_op jit(solution)/shard_map/dot_general | solution.py:168
  777.1 23.8 %out_and_down.8 = (bf16[2,128,2560]{2,1,0:T(8,128)(2,1)}, bf16[2,128,2560]{2,1,0:T(8,128)(2,1)}, bf16[2,128,2560]{2,1,0:T(8,128)(2,1)}, bf16[2,128,2560]{2,1,0:T(8,128)(2,1)}, bf16[2,128,2560]{2,1,0:T(8,128)(2,1)}) custom-call(s32[1]{0:T(128)} %bitcast.1.rank_ref, bf16[1024,640]{1,0:T(8,128)(2,1)} %reshape.521.o_ref, bf16[1024,2560]{1,0:T(8,128)(2,1)} %fusion.34.g_ref, ...), custom_call_target="tpu_custom_call" | custom-call | flops 16777216000 | bytes 28180480 | tf_op jit(solution)/shard_map/out_and_down/pallas_call | solution.py:91
  814.6 17.3 collective-permute-done.6
  839.9 20.0 collective-permute-done.40
  872.5 15.5 collective-permute-done.29
  947.1 17.1 collective-permute-start.19
  984.5 15.8 collective-permute-done.30
  1004.8 23.6 %collective-permute-done.19 = bf16[2,128,2560]{2,1,0:T(8,128)(2,1)S(1)} collective-permute-done((bf16[2,128,2560]{2,1,0:T(8,128)(2,1)S(1)}, bf16[2,128,2560]{2,1,0:T(8,128)(2,1)S(1)}, u32[]{:S(2)}, u32[]{:S(2)}) %collective-permute-start.19) | collective-permute-done | bytes 1310752 | tf_op jit(solution)/shard_map/ppermute | solution.py:125
  1036.9 19.5 collective-permute-done.8
  1064.6 19.9 collective-permute-done.87.refs_1_
  1095.5 17.2 collective-permute-done.72.refs_1_
  1122.4 25.7 %collective-permute-done.75.refs_4_ = bf16[2,128,2560]{2,1,0:T(8,128)(2,1)} collective-permute-done((bf16[2,128,2560]{2,1,0:T(8,128)(2,1)S(1)}, bf16[2,128,2560]{2,1,0:T(8,128)(2,1)}, u32[]{:S(2)}, u32[]{:S(2)}) %collective-permute-start.75) | collective-permute-done | bytes 1310752 | tf_op jit(solution)/shard_map/ppermute | solution.py:115
  1153.4 22.7 %collective-permute-done.63.refs_4_ = bf16[2,128,2560]{2,1,0:T(8,128)(2,1)S(1)} collective-permute-done((bf16[2,128,2560]{2,1,0:T(8,128)(2,1)S(1)}, bf16[2,128,2560]{2,1,0:T(8,128)(2,1)S(1)}, u32[]{:S(2)}, u32[]{:S(2)}) %collective-permute-start.63) | collective-permute-done | bytes 1310752 | tf_op jit(solution)/shard_map/ppermute | solution.py:115
  1185.3 18.9 collective-permute-done.92.refs_6_
  1235.4 25.1 %collective-permute-done.76.refs_5_ = bf16[2,128,2560]{2,1,0:T(8,128)(2,1)} collective-permute-done((bf16[2,128,2560]{2,1,0:T(8,128)(2,1)}, bf16[2,128,2560]{2,1,0:T(8,128)(2,1)}, u32[]{:S(2)}, u32[]{:S(2)}) %collective-permute-start.76) | collective-permute-done | bytes 1310752 | tf_op jit(solution)/shard_map/ppermute | solution.py:115
  1262.5 16.1 fusion.187
  1291.6 25.1 %collective-permute-done.52.refs_5_ = bf16[2,128,2560]{2,1,0:T(8,128)(2,1)} collective-permute-done((bf16[2,128,2560]{2,1,0:T(8,128)(2,1)}, bf16[2,128,2560]{2,1,0:T(8,128)(2,1)}, u32[]{:S(2)}, u32[]{:S(2)}) %collective-permute-start.52) | collective-permute-done | bytes 1310752 | tf_op jit(solution)/shard_map/ppermute | solution.py:115
  1319.9 24.8 %collective-permute-done.77.refs_6_ = bf16[2,128,2560]{2,1,0:T(8,128)(2,1)} collective-permute-done((bf16[2,128,2560]{2,1,0:T(8,128)(2,1)}, bf16[2,128,2560]{2,1,0:T(8,128)(2,1)}, u32[]{:S(2)}, u32[]{:S(2)}) %collective-permute-start.77) | collective-permute-done | bytes 1310752 | tf_op jit(solution)/shard_map/ppermute | solution.py:115
  1481.0 39.7 %fusion.55.g_ref = bf16[1024,2560]{1,0:T(8,128)(2,1)} fusion(bf16[1024,2560]{1,0:T(8,128)(2,1)} %bitcast.706, bf16[1,2560,2560]{2,1,0:T(8,128)(2,1)} %param.16), kind=kOutput, calls=%fused_computation.88 | convolution fusion | flops 13592166400 | bytes 23592960 | tf_op jit(solution)/shard_map/dot_general | solution.py:168
  1520.8 23.8 %out_and_down.15 = (bf16[2,128,2560]{2,1,0:T(8,128)(2,1)}, bf16[2,128,2560]{2,1,0:T(8,128)(2,1)}, bf16[2,128,2560]{2,1,0:T(8,128)(2,1)}, bf16[2,128,2560]{2,1,0:T(8,128)(2,1)}, bf16[2,128,2560]{2,1,0:T(8,128)(2,1)}) custom-call(s32[1]{0:T(128)} %bitcast.1.rank_ref, bf16[1024,640]{1,0:T(8,128)(2,1)} %reshape.528.o_ref, bf16[1024,2560]{1,0:T(8,128)(2,1)} %fusion.55.g_ref, ...), custom_call_target="tpu_custom_call" | custom-call | flops 16777216000 | bytes 28180480 | tf_op jit(solution)/shard_map/out_and_down/pallas_call | solution.py:91
  1579.7 40.0 %fusion.52.g_ref = bf16[1024,2560]{1,0:T(8,128)(2,1)} fusion(bf16[1024,2560]{1,0:T(8,128)(2,1)} %bitcast.713, bf16[1,2560,2560]{2,1,0:T(8,128)(2,1)} %param.16), kind=kOutput, calls=%fused_computation.85 | convolution fusion | flops 13592166400 | bytes 23592960 | tf_op jit(solution)/shard_map/dot_general | solution.py:168
  1619.7 23.8 %out_and_down.14 = (bf16[2,128,2560]{2,1,0:T(8,128)(2,1)}, bf16[2,128,2560]{2,1,0:T(8,128)(2,1)}, bf16[2,128,2560]{2,1,0:T(8,128)(2,1)}, bf16[2,128,2560]{2,1,0:T(8,128)(2,1)}, bf16[2,128,2560]{2,1,0:T(8,128)(2,1)}) custom-call(s32[1]{0:T(128)} %bitcast.1.rank_ref, bf16[1024,640]{1,0:T(8,128)(2,1)} %reshape.527.o_ref, bf16[1024,2560]{1,0:T(8,128)(2,1)} %fusion.52.g_ref, ...), custom_call_target="tpu_custom_call" | custom-call | flops 16777216000 | bytes 28180480 | tf_op jit(solution)/shard_map/out_and_down/pallas_call | solution.py:91
  1678.2 39.7 %fusion.49.g_ref = bf16[1024,2560]{1,0:T(8,128)(2,1)} fusion(bf16[1024,2560]{1,0:T(8,128)(2,1)} %bitcast.709, bf16[1,2560,2560]{2,1,0:T(8,128)(2,1)} %param.16), kind=kOutput, calls=%fused_computation.82 | convolution fusion | flops 13592166400 | bytes 23592960 | tf_op jit(solution)/shard_map/dot_general | solution.py:168
  1717.9 23.8 %out_and_down.13 = (bf16[2,128,2560]{2,1,0:T(8,128)(2,1)}, bf16[2,128,2560]{2,1,0:T(8,128)(2,1)}, bf16[2,128,2560]{2,1,0:T(8,128)(2,1)}, bf16[2,128,2560]{2,1,0:T(8,128)(2,1)}, bf16[2,128,2560]{2,1,0:T(8,128)(2,1)}) custom-call(s32[1]{0:T(128)} %bitcast.1.rank_ref, bf16[1024,640]{1,0:T(8,128)(2,1)} %reshape.526.o_ref, bf16[1024,2560]{1,0:T(8,128)(2,1)} %fusion.49.g_ref, ...), custom_call_target="tpu_custom_call" | custom-call | flops 16777216000 | bytes 28180480 | tf_op jit(solution)/shard_map/out_and_down/pallas_call | solution.py:91
  1774.2 40.0 %fusion.46.g_ref = bf16[1024,2560]{1,0:T(8,128)(2,1)} fusion(bf16[1024,2560]{1,0:T(8,128)(2,1)} %bitcast.707, bf16[1,2560,2560]{2,1,0:T(8,128)(2,1)} %param.16), kind=kOutput, calls=%fused_computation.79 | convolution fusion | flops 13592166400 | bytes 23592960 | tf_op jit(solution)/shard_map/dot_general | solution.py:168
  1814.2 23.8 %out_and_down.12 = (bf16[2,128,2560]{2,1,0:T(8,128)(2,1)}, bf16[2,128,2560]{2,1,0:T(8,128)(2,1)}, bf16[2,128,2560]{2,1,0:T(8,128)(2,1)}, bf16[2,128,2560]{2,1,0:T(8,128)(2,1)}, bf16[2,128,2560]{2,1,0:T(8,128)(2,1)}) custom-call(s32[1]{0:T(128)} %bitcast.1.rank_ref, bf16[1024,640]{1,0:T(8,128)(2,1)} %reshape.525.o_ref, bf16[1024,2560]{1,0:T(8,128)(2,1)} %fusion.46.g_ref, ...), custom_call_target="tpu_custom_call" | custom-call | flops 16777216000 | bytes 28180480 | tf_op jit(solution)/shard_map/out_and_down/pallas_call | solution.py:91
  1848.8 20.1 collective-permute-done.54
  1875.7 21.2 collective-permute-done.79
  1904.8 20.2 collective-permute-done.67
  1935.9 17.2 collective-permute-done.94
  1960.9 20.2 collective-permute-done.55
  1984.2 25.0 %collective-permute-done.80 = bf16[2,128,2560]{2,1,0:T(8,128)(2,1)S(1)} collective-permute-done((bf16[2,128,2560]{2,1,0:T(8,128)(2,1)S(1)}, bf16[2,128,2560]{2,1,0:T(8,128)(2,1)S(1)}, u32[]{:S(2)}, u32[]{:S(2)}) %collective-permute-start.80) | collective-permute-done | bytes 1310752 | tf_op jit(solution)/shard_map/ppermute | solution.py:125
  2015.2 20.5 collective-permute-done.68
  (609 shorter events, 983.1 us)
Async XLA Ops:
  15.5 77.1 %collective-permute-start.11 = (bf16[2,128,2560]{2,1,0:T(8,128)(2,1)S(1)}, bf16[2,128,2560]{2,1,0:T(8,128)(2,1)}, u32[]{:S(2)}, u32[]{:S(2)}) collective-permute-start(bf16[2,128,2560]{2,1,0:T(8,128)(2,1)S(1)} %get-tuple-element.165.refs_0_), channel_id=1, source_target_pairs={{0,4},{4,8},{8,12},{1,5},{5,9},{9,13},{2,6},{6,10},{10,14},{3,7},{... | collective-permute-start | bytes 3932168 | tf_op jit(solution)/shard_map/ppermute | solution.py:114
  40.9 78.7 %collective-permute-start = (bf16[2,128,2560]{2,1,0:T(8,128)(2,1)S(1)}, bf16[2,128,2560]{2,1,0:T(8,128)(2,1)S(1)}, u32[]{:S(2)}, u32[]{:S(2)}) collective-permute-start(bf16[2,128,2560]{2,1,0:T(8,128)(2,1)S(1)} %get-tuple-element.149.refs_0_), channel_id=1, source_target_pairs={{0,4},{4,8},{8,12},{1,5},{5,9},{9,13},{2,6},{6,10},{10,14},{3,7},{... | collective-permute-start | bytes 3932168 | tf_op jit(solution)/shard_map/ppermute | solution.py:114
  97.1 61.9 %collective-permute-start.23 = (bf16[2,128,2560]{2,1,0:T(8,128)(2,1)}, bf16[2,128,2560]{2,1,0:T(8,128)(2,1)}, u32[]{:S(2)}, u32[]{:S(2)}) collective-permute-start(bf16[2,128,2560]{2,1,0:T(8,128)(2,1)} %collective-permute-done.22.refs_1_), channel_id=1, source_target_pairs={{4,8},{8,12},{5,9},{9,13},{6,10},{10,14},{7,11},{11,15},{20,24},{2... | collective-permute-start | bytes 3932168 | tf_op jit(solution)/shard_map/ppermute | solution.py:114
  119.6 61.9 %collective-permute-start.26 = (bf16[2,128,2560]{2,1,0:T(8,128)(2,1)}, bf16[2,128,2560]{2,1,0:T(8,128)(2,1)}, u32[]{:S(2)}, u32[]{:S(2)}) collective-permute-start(bf16[2,128,2560]{2,1,0:T(8,128)(2,1)} %collective-permute-done.25.refs_4_), channel_id=1, source_target_pairs={{4,0},{8,4},{5,1},{9,5},{6,2},{10,6},{7,3},{11,7},{20,16},{24,20},... | collective-permute-start | bytes 3932168 | tf_op jit(solution)/shard_map/ppermute | solution.py:115
  158.9 78.7 %collective-permute-start.15 = (bf16[2,128,2560]{2,1,0:T(8,128)(2,1)}, bf16[2,128,2560]{2,1,0:T(8,128)(2,1)}, u32[]{:S(2)}, u32[]{:S(2)}) collective-permute-start(bf16[2,128,2560]{2,1,0:T(8,128)(2,1)} %copy-done.125), channel_id=1, source_target_pairs={{4,0},{8,4},{5,1},{9,5},{6,2},{10,6},{7,3},{11,7},{20,16},{24,20},... | collective-permute-start | bytes 3932168 | tf_op jit(solution)/shard_map/ppermute | solution.py:115
  183.1 82.6 %collective-permute-start.4 = (bf16[2,128,2560]{2,1,0:T(8,128)(2,1)}, bf16[2,128,2560]{2,1,0:T(8,128)(2,1)}, u32[]{:S(2)}, u32[]{:S(2)}) collective-permute-start(bf16[2,128,2560]{2,1,0:T(8,128)(2,1)} %copy-done.124), channel_id=1, source_target_pairs={{4,0},{8,4},{5,1},{9,5},{6,2},{10,6},{7,3},{11,7},{20,16},{24,20},... | collective-permute-start | bytes 3932168 | tf_op jit(solution)/shard_map/ppermute | solution.py:115
  184.4 83.0 %collective-permute-start.24 = (bf16[2,128,2560]{2,1,0:T(8,128)(2,1)}, bf16[2,128,2560]{2,1,0:T(8,128)(2,1)}, u32[]{:S(2)}, u32[]{:S(2)}) collective-permute-start(bf16[2,128,2560]{2,1,0:T(8,128)(2,1)} %collective-permute-done.23.refs_2_), channel_id=1, source_target_pairs={{8,12},{9,13},{10,14},{11,15},{24,28},{25,29},{26,30},{27,31}} | collective-permute-start | bytes 3932168 | tf_op jit(solution)/shard_map/ppermute | solution.py:114
  209.5 84.3 %collective-permute-start.27 = (bf16[2,128,2560]{2,1,0:T(8,128)(2,1)}, bf16[2,128,2560]{2,1,0:T(8,128)(2,1)}, u32[]{:S(2)}, u32[]{:S(2)}) collective-permute-start(bf16[2,128,2560]{2,1,0:T(8,128)(2,1)} %collective-permute-done.26.refs_5_), channel_id=1, source_target_pairs={{4,0},{5,1},{6,2},{7,3},{20,16},{21,17},{22,18},{23,19}} | collective-permute-start | bytes 3932168 | tf_op jit(solution)/shard_map/ppermute | solution.py:115
  237.6 106.7 %collective-permute-start.13 = (bf16[2,128,2560]{2,1,0:T(8,128)(2,1)}, bf16[2,128,2560]{2,1,0:T(8,128)(2,1)}, u32[]{:S(2)}, u32[]{:S(2)}) collective-permute-start(bf16[2,128,2560]{2,1,0:T(8,128)(2,1)} %collective-permute-done.12.refs_2_), channel_id=1, source_target_pairs={{8,12},{9,13},{10,14},{11,15},{24,28},{25,29},{26,30},{27,31}} | collective-permute-start | bytes 3932168 | tf_op jit(solution)/shard_map/ppermute | solution.py:114
  239.3 105.0 %collective-permute-start.16 = (bf16[2,128,2560]{2,1,0:T(8,128)(2,1)}, bf16[2,128,2560]{2,1,0:T(8,128)(2,1)}, u32[]{:S(2)}, u32[]{:S(2)}) collective-permute-start(bf16[2,128,2560]{2,1,0:T(8,128)(2,1)} %collective-permute-done.15.refs_5_), channel_id=1, source_target_pairs={{4,0},{5,1},{6,2},{7,3},{20,16},{21,17},{22,18},{23,19}} | collective-permute-start | bytes 3932168 | tf_op jit(solution)/shard_map/ppermute | solution.py:115
  265.7 114.1 %collective-permute-start.2 = (bf16[2,128,2560]{2,1,0:T(8,128)(2,1)}, bf16[2,128,2560]{2,1,0:T(8,128)(2,1)}, u32[]{:S(2)}, u32[]{:S(2)}) collective-permute-start(bf16[2,128,2560]{2,1,0:T(8,128)(2,1)} %collective-permute-done.1.refs_2_), channel_id=1, source_target_pairs={{8,12},{9,13},{10,14},{11,15},{24,28},{25,29},{26,30},{27,31}} | collective-permute-start | bytes 3932168 | tf_op jit(solution)/shard_map/ppermute | solution.py:114
  267.4 112.4 %collective-permute-start.5 = (bf16[2,128,2560]{2,1,0:T(8,128)(2,1)}, bf16[2,128,2560]{2,1,0:T(8,128)(2,1)}, u32[]{:S(2)}, u32[]{:S(2)}) collective-permute-start(bf16[2,128,2560]{2,1,0:T(8,128)(2,1)} %collective-permute-done.4.refs_5_), channel_id=1, source_target_pairs={{4,0},{5,1},{6,2},{7,3},{20,16},{21,17},{22,18},{23,19}} | collective-permute-start | bytes 3932168 | tf_op jit(solution)/shard_map/ppermute | solution.py:115
  507.7 294.7 %collective-permute-start.39 = (bf16[2,128,2560]{2,1,0:T(8,128)(2,1)}, bf16[2,128,2560]{2,1,0:T(8,128)(2,1)}, u32[]{:S(2)}, u32[]{:S(2)}) collective-permute-start(bf16[2,128,2560]{2,1,0:T(8,128)(2,1)} %get-tuple-element.201), channel_id=1, source_target_pairs={{0,4},{12,8},{1,5},{13,9},{2,6},{14,10},{3,7},{15,11},{16,20},{28,... | collective-permute-start | bytes 3932168 | tf_op jit(solution)/shard_map/ppermute | solution.py:120
  606.5 199.9 %collective-permute-start.28 = (bf16[2,128,2560]{2,1,0:T(8,128)(2,1)}, bf16[2,128,2560]{2,1,0:T(8,128)(2,1)}, u32[]{:S(2)}, u32[]{:S(2)}) collective-permute-start(bf16[2,128,2560]{2,1,0:T(8,128)(2,1)} %get-tuple-element.185), channel_id=1, source_target_pairs={{0,4},{12,8},{1,5},{13,9},{2,6},{14,10},{3,7},{15,11},{16,20},{28,... | collective-permute-start | bytes 3932168 | tf_op jit(solution)/shard_map/ppermute | solution.py:120
  704.8 104.3 %collective-permute-start.17 = (bf16[2,128,2560]{2,1,0:T(8,128)(2,1)}, bf16[2,128,2560]{2,1,0:T(8,128)(2,1)}, u32[]{:S(2)}, u32[]{:S(2)}) collective-permute-start(bf16[2,128,2560]{2,1,0:T(8,128)(2,1)} %get-tuple-element.169), channel_id=1, source_target_pairs={{0,4},{12,8},{1,5},{13,9},{2,6},{14,10},{3,7},{15,11},{16,20},{28,... | collective-permute-start | bytes 3932168 | tf_op jit(solution)/shard_map/ppermute | solution.py:120
  809.1 78.8 %collective-permute-start.29 = (bf16[2,128,2560]{2,1,0:T(8,128)(2,1)S(1)}, bf16[2,128,2560]{2,1,0:T(8,128)(2,1)S(1)}, u32[]{:S(2)}, u32[]{:S(2)}) collective-permute-start(bf16[2,128,2560]{2,1,0:T(8,128)(2,1)S(1)} %add.306), channel_id=1, source_target_pairs={{0,4},{4,8},{1,5},{5,9},{2,6},{6,10},{3,7},{7,11},{16,20},{20,24},... | collective-permute-start | bytes 3932168 | tf_op jit(solution)/shard_map/ppermute | solution.py:122
  835.0 81.1 %collective-permute-start.18 = (bf16[2,128,2560]{2,1,0:T(8,128)(2,1)}, bf16[2,128,2560]{2,1,0:T(8,128)(2,1)}, u32[]{:S(2)}, u32[]{:S(2)}) collective-permute-start(bf16[2,128,2560]{2,1,0:T(8,128)(2,1)} %add.298), channel_id=1, source_target_pairs={{0,4},{4,8},{1,5},{5,9},{2,6},{6,10},{3,7},{7,11},{16,20},{20,24},... | collective-permute-start | bytes 3932168 | tf_op jit(solution)/shard_map/ppermute | solution.py:122
  862.9 81.2 %collective-permute-start.7 = (bf16[2,128,2560]{2,1,0:T(8,128)(2,1)}, bf16[2,128,2560]{2,1,0:T(8,128)(2,1)}, u32[]{:S(2)}, u32[]{:S(2)}) collective-permute-start(bf16[2,128,2560]{2,1,0:T(8,128)(2,1)} %add.290), channel_id=1, source_target_pairs={{0,4},{4,8},{1,5},{5,9},{2,6},{6,10},{3,7},{7,11},{16,20},{20,24},... | collective-permute-start | bytes 3932168 | tf_op jit(solution)/shard_map/ppermute | solution.py:122
  890.2 82.0 %collective-permute-start.41 = (bf16[2,128,2560]{2,1,0:T(8,128)(2,1)}, bf16[2,128,2560]{2,1,0:T(8,128)(2,1)}, u32[]{:S(2)}, u32[]{:S(2)}) collective-permute-start(bf16[2,128,2560]{2,1,0:T(8,128)(2,1)} %add.315), channel_id=1, source_target_pairs={{0,4},{4,8},{8,12},{1,5},{5,9},{9,13},{2,6},{6,10},{10,14},{3,7},{... | collective-permute-start | bytes 3932168 | tf_op jit(solution)/shard_map/ppermute | solution.py:125
  917.4 82.9 %collective-permute-start.30 = (bf16[2,128,2560]{2,1,0:T(8,128)(2,1)S(1)}, bf16[2,128,2560]{2,1,0:T(8,128)(2,1)S(1)}, u32[]{:S(2)}, u32[]{:S(2)}) collective-permute-start(bf16[2,128,2560]{2,1,0:T(8,128)(2,1)S(1)} %add.307), channel_id=1, source_target_pairs={{0,4},{4,8},{8,12},{1,5},{5,9},{9,13},{2,6},{6,10},{10,14},{3,7},{... | collective-permute-start | bytes 3932168 | tf_op jit(solution)/shard_map/ppermute | solution.py:125
  947.1 81.2 %collective-permute-start.19 = (bf16[2,128,2560]{2,1,0:T(8,128)(2,1)S(1)}, bf16[2,128,2560]{2,1,0:T(8,128)(2,1)S(1)}, u32[]{:S(2)}, u32[]{:S(2)}) collective-permute-start(bf16[2,128,2560]{2,1,0:T(8,128)(2,1)S(1)} %add.299), channel_id=1, source_target_pairs={{0,4},{4,8},{8,12},{1,5},{5,9},{9,13},{2,6},{6,10},{10,14},{3,7},{... | collective-permute-start | bytes 3932168 | tf_op jit(solution)/shard_map/ppermute | solution.py:125
  972.3 63.3 %collective-permute-start.10 = (bf16[2,128,2560]{2,1,0:T(8,128)(2,1)S(1)}, bf16[2,128,2560]{2,1,0:T(8,128)(2,1)S(1)}, u32[]{:S(2)}, u32[]{:S(2)}) collective-permute-start(bf16[2,128,2560]{2,1,0:T(8,128)(2,1)S(1)} %add.293), channel_id=1, source_target_pairs={{12,8},{8,4},{4,0},{13,9},{9,5},{5,1},{14,10},{10,6},{6,2},{15,11}... | collective-permute-start | bytes 3932168 | tf_op jit(solution)/shard_map/ppermute | solution.py:126
  976.0 80.5 %collective-permute-start.8 = (bf16[2,128,2560]{2,1,0:T(8,128)(2,1)S(1)}, bf16[2,128,2560]{2,1,0:T(8,128)(2,1)S(1)}, u32[]{:S(2)}, u32[]{:S(2)}) collective-permute-start(bf16[2,128,2560]{2,1,0:T(8,128)(2,1)S(1)} %add.291), channel_id=1, source_target_pairs={{0,4},{4,8},{8,12},{1,5},{5,9},{9,13},{2,6},{6,10},{10,14},{3,7},{... | collective-permute-start | bytes 3932168 | tf_op jit(solution)/shard_map/ppermute | solution.py:125
  1086.6 61.5 %collective-permute-start.75 = (bf16[2,128,2560]{2,1,0:T(8,128)(2,1)S(1)}, bf16[2,128,2560]{2,1,0:T(8,128)(2,1)}, u32[]{:S(2)}, u32[]{:S(2)}) collective-permute-start(bf16[2,128,2560]{2,1,0:T(8,128)(2,1)S(1)} %broadcast_select_fusion.1.refs_0_), channel_id=1, source_target_pairs={{4,0},{8,4},{12,8},{5,1},{9,5},{13,9},{6,2},{10,6},{14,10},{7,3},{... | collective-permute-start | bytes 3932168 | tf_op jit(solution)/shard_map/ppermute | solution.py:115
  1088.1 64.1 %collective-permute-start.60 = (bf16[2,128,2560]{2,1,0:T(8,128)(2,1)S(1)}, bf16[2,128,2560]{2,1,0:T(8,128)(2,1)}, u32[]{:S(2)}, u32[]{:S(2)}) collective-permute-start(bf16[2,128,2560]{2,1,0:T(8,128)(2,1)S(1)} %broadcast_select_fusion.2.refs_0_), channel_id=1, source_target_pairs={{0,4},{4,8},{8,12},{1,5},{5,9},{9,13},{2,6},{6,10},{10,14},{3,7},{... | collective-permute-start | bytes 3932168 | tf_op jit(solution)/shard_map/ppermute | solution.py:114
  1112.6 63.5 %collective-permute-start.63 = (bf16[2,128,2560]{2,1,0:T(8,128)(2,1)S(1)}, bf16[2,128,2560]{2,1,0:T(8,128)(2,1)S(1)}, u32[]{:S(2)}, u32[]{:S(2)}) collective-permute-start(bf16[2,128,2560]{2,1,0:T(8,128)(2,1)S(1)} %broadcast_select_fusion.2.refs_0_), channel_id=1, source_target_pairs={{4,0},{8,4},{12,8},{5,1},{9,5},{13,9},{6,2},{10,6},{14,10},{7,3},{... | collective-permute-start | bytes 3932168 | tf_op jit(solution)/shard_map/ppermute | solution.py:115
  1113.9 63.9 %collective-permute-start.89 = (bf16[2,128,2560]{2,1,0:T(8,128)(2,1)S(1)}, bf16[2,128,2560]{2,1,0:T(8,128)(2,1)S(1)}, u32[]{:S(2)}, u32[]{:S(2)}) collective-permute-start(bf16[2,128,2560]{2,1,0:T(8,128)(2,1)S(1)} %collective-permute-done.88.refs_2_), channel_id=1, source_target_pairs={{8,12},{9,13},{10,14},{11,15},{24,28},{25,29},{26,30},{27,31}} | collective-permute-start | bytes 3932168 | tf_op jit(solution)/shard_map/ppermute | solution.py:114
  1119.9 84.3 %collective-permute-start.92 = (bf16[2,128,2560]{2,1,0:T(8,128)(2,1)S(1)}, bf16[2,128,2560]{2,1,0:T(8,128)(2,1)S(1)}, u32[]{:S(2)}, u32[]{:S(2)}) collective-permute-start(bf16[2,128,2560]{2,1,0:T(8,128)(2,1)S(1)} %collective-permute-done.91.refs_5_), channel_id=1, source_target_pairs={{4,0},{5,1},{6,2},{7,3},{20,16},{21,17},{22,18},{23,19}} | collective-permute-start | bytes 3932168 | tf_op jit(solution)/shard_map/ppermute | solution.py:115
  1148.1 72.4 %collective-permute-start.48 = (bf16[2,128,2560]{2,1,0:T(8,128)(2,1)}, bf16[2,128,2560]{2,1,0:T(8,128)(2,1)S(1)}, u32[]{:S(2)}, u32[]{:S(2)}) collective-permute-start(bf16[2,128,2560]{2,1,0:T(8,128)(2,1)} %broadcast_select_fusion.3.refs_0_), channel_id=1, source_target_pairs={{0,4},{4,8},{8,12},{1,5},{5,9},{9,13},{2,6},{6,10},{10,14},{3,7},{... | collective-permute-start | bytes 3932168 | tf_op jit(solution)/shard_map/ppermute | solution.py:114
  1152.1 80.3 %collective-permute-start.51 = (bf16[2,128,2560]{2,1,0:T(8,128)(2,1)}, bf16[2,128,2560]{2,1,0:T(8,128)(2,1)}, u32[]{:S(2)}, u32[]{:S(2)}) collective-permute-start(bf16[2,128,2560]{2,1,0:T(8,128)(2,1)} %broadcast_select_fusion.3.refs_0_), channel_id=1, source_target_pairs={{4,0},{8,4},{12,8},{5,1},{9,5},{13,9},{6,2},{10,6},{14,10},{7,3},{... | collective-permute-start | bytes 3932168 | tf_op jit(solution)/shard_map/ppermute | solution.py:115
  1177.8 82.6 %collective-permute-start.76 = (bf16[2,128,2560]{2,1,0:T(8,128)(2,1)}, bf16[2,128,2560]{2,1,0:T(8,128)(2,1)}, u32[]{:S(2)}, u32[]{:S(2)}) collective-permute-start(bf16[2,128,2560]{2,1,0:T(8,128)(2,1)} %collective-permute-done.75.refs_4_), channel_id=1, source_target_pairs={{4,0},{8,4},{5,1},{9,5},{6,2},{10,6},{7,3},{11,7},{20,16},{24,20},... | collective-permute-start | bytes 3932168 | tf_op jit(solution)/shard_map/ppermute | solution.py:115
  1220.6 68.0 %collective-permute-start.64 = (bf16[2,128,2560]{2,1,0:T(8,128)(2,1)}, bf16[2,128,2560]{2,1,0:T(8,128)(2,1)}, u32[]{:S(2)}, u32[]{:S(2)}) collective-permute-start(bf16[2,128,2560]{2,1,0:T(8,128)(2,1)} %copy-done.127), channel_id=1, source_target_pairs={{4,0},{8,4},{5,1},{9,5},{6,2},{10,6},{7,3},{11,7},{20,16},{24,20},... | collective-permute-start | bytes 3932168 | tf_op jit(solution)/shard_map/ppermute | solution.py:115
  1234.1 82.5 %collective-permute-start.52 = (bf16[2,128,2560]{2,1,0:T(8,128)(2,1)}, bf16[2,128,2560]{2,1,0:T(8,128)(2,1)}, u32[]{:S(2)}, u32[]{:S(2)}) collective-permute-start(bf16[2,128,2560]{2,1,0:T(8,128)(2,1)} %collective-permute-done.51.refs_4_), channel_id=1, source_target_pairs={{4,0},{8,4},{5,1},{9,5},{6,2},{10,6},{7,3},{11,7},{20,16},{24,20},... | collective-permute-start | bytes 3932168 | tf_op jit(solution)/shard_map/ppermute | solution.py:115
  1261.2 83.5 %collective-permute-start.77 = (bf16[2,128,2560]{2,1,0:T(8,128)(2,1)}, bf16[2,128,2560]{2,1,0:T(8,128)(2,1)}, u32[]{:S(2)}, u32[]{:S(2)}) collective-permute-start(bf16[2,128,2560]{2,1,0:T(8,128)(2,1)} %collective-permute-done.76.refs_5_), channel_id=1, source_target_pairs={{4,0},{5,1},{6,2},{7,3},{20,16},{21,17},{22,18},{23,19}} | collective-permute-start | bytes 3932168 | tf_op jit(solution)/shard_map/ppermute | solution.py:115
  1288.6 92.2 %collective-permute-start.62 = (bf16[2,128,2560]{2,1,0:T(8,128)(2,1)}, bf16[2,128,2560]{2,1,0:T(8,128)(2,1)}, u32[]{:S(2)}, u32[]{:S(2)}) collective-permute-start(bf16[2,128,2560]{2,1,0:T(8,128)(2,1)} %collective-permute-done.61.refs_2_), channel_id=1, source_target_pairs={{8,12},{9,13},{10,14},{11,15},{24,28},{25,29},{26,30},{27,31}} | collective-permute-start | bytes 3932168 | tf_op jit(solution)/shard_map/ppermute | solution.py:114
  1290.3 90.5 %collective-permute-start.65 = (bf16[2,128,2560]{2,1,0:T(8,128)(2,1)}, bf16[2,128,2560]{2,1,0:T(8,128)(2,1)}, u32[]{:S(2)}, u32[]{:S(2)}) collective-permute-start(bf16[2,128,2560]{2,1,0:T(8,128)(2,1)} %collective-permute-done.64.refs_5_), channel_id=1, source_target_pairs={{4,0},{5,1},{6,2},{7,3},{20,16},{21,17},{22,18},{23,19}} | collective-permute-start | bytes 3932168 | tf_op jit(solution)/shard_map/ppermute | solution.py:115
  1316.7 99.5 %collective-permute-start.50 = (bf16[2,128,2560]{2,1,0:T(8,128)(2,1)}, bf16[2,128,2560]{2,1,0:T(8,128)(2,1)}, u32[]{:S(2)}, u32[]{:S(2)}) collective-permute-start(bf16[2,128,2560]{2,1,0:T(8,128)(2,1)} %collective-permute-done.49.refs_2_), channel_id=1, source_target_pairs={{8,12},{9,13},{10,14},{11,15},{24,28},{25,29},{26,30},{27,31}} | collective-permute-start | bytes 3932168 | tf_op jit(solution)/shard_map/ppermute | solution.py:114
  1318.5 97.7 %collective-permute-start.53 = (bf16[2,128,2560]{2,1,0:T(8,128)(2,1)}, bf16[2,128,2560]{2,1,0:T(8,128)(2,1)}, u32[]{:S(2)}, u32[]{:S(2)}) collective-permute-start(bf16[2,128,2560]{2,1,0:T(8,128)(2,1)} %collective-permute-done.52.refs_5_), channel_id=1, source_target_pairs={{4,0},{5,1},{6,2},{7,3},{20,16},{21,17},{22,18},{23,19}} | collective-permute-start | bytes 3932168 | tf_op jit(solution)/shard_map/ppermute | solution.py:115
  1544.6 298.8 %collective-permute-start.93 = (bf16[2,128,2560]{2,1,0:T(8,128)(2,1)}, bf16[2,128,2560]{2,1,0:T(8,128)(2,1)}, u32[]{:S(2)}, u32[]{:S(2)}) collective-permute-start(bf16[2,128,2560]{2,1,0:T(8,128)(2,1)} %get-tuple-element.273), channel_id=1, source_target_pairs={{0,4},{12,8},{1,5},{13,9},{2,6},{14,10},{3,7},{15,11},{16,20},{28,... | collective-permute-start | bytes 3932168 | tf_op jit(solution)/shard_map/ppermute | solution.py:120
  1643.5 196.0 %collective-permute-start.78 = (bf16[2,128,2560]{2,1,0:T(8,128)(2,1)}, bf16[2,128,2560]{2,1,0:T(8,128)(2,1)}, u32[]{:S(2)}, u32[]{:S(2)}) collective-permute-start(bf16[2,128,2560]{2,1,0:T(8,128)(2,1)} %get-tuple-element.255), channel_id=1, source_target_pairs={{0,4},{12,8},{1,5},{13,9},{2,6},{14,10},{3,7},{15,11},{16,20},{28,... | collective-permute-start | bytes 3932168 | tf_op jit(solution)/shard_map/ppermute | solution.py:120
  1741.7 104.5 %collective-permute-start.66 = (bf16[2,128,2560]{2,1,0:T(8,128)(2,1)}, bf16[2,128,2560]{2,1,0:T(8,128)(2,1)}, u32[]{:S(2)}, u32[]{:S(2)}) collective-permute-start(bf16[2,128,2560]{2,1,0:T(8,128)(2,1)} %get-tuple-element.237), channel_id=1, source_target_pairs={{0,4},{12,8},{1,5},{13,9},{2,6},{14,10},{3,7},{15,11},{16,20},{28,... | collective-permute-start | bytes 3932168 | tf_op jit(solution)/shard_map/ppermute | solution.py:120
  1873.6 79.4 %collective-permute-start.94 = (bf16[2,128,2560]{2,1,0:T(8,128)(2,1)S(1)}, bf16[2,128,2560]{2,1,0:T(8,128)(2,1)S(1)}, u32[]{:S(2)}, u32[]{:S(2)}) collective-permute-start(bf16[2,128,2560]{2,1,0:T(8,128)(2,1)S(1)} %add.352), channel_id=1, source_target_pairs={{0,4},{4,8},{1,5},{5,9},{2,6},{6,10},{3,7},{7,11},{16,20},{20,24},... | collective-permute-start | bytes 3932168 | tf_op jit(solution)/shard_map/ppermute | solution.py:122
  1898.3 82.8 %collective-permute-start.55 = (bf16[2,128,2560]{2,1,0:T(8,128)(2,1)S(1)}, bf16[2,128,2560]{2,1,0:T(8,128)(2,1)S(1)}, u32[]{:S(2)}, u32[]{:S(2)}) collective-permute-start(bf16[2,128,2560]{2,1,0:T(8,128)(2,1)S(1)} %add.325), channel_id=1, source_target_pairs={{0,4},{4,8},{1,5},{5,9},{2,6},{6,10},{3,7},{7,11},{16,20},{20,24},... | collective-permute-start | bytes 3932168 | tf_op jit(solution)/shard_map/ppermute | solution.py:122
  1903.5 79.3 %collective-permute-start.82 = (bf16[2,128,2560]{2,1,0:T(8,128)(2,1)S(1)}, bf16[2,128,2560]{2,1,0:T(8,128)(2,1)S(1)}, u32[]{:S(2)}, u32[]{:S(2)}) collective-permute-start(bf16[2,128,2560]{2,1,0:T(8,128)(2,1)S(1)} %add.344), channel_id=1, source_target_pairs={{12,8},{8,4},{4,0},{13,9},{9,5},{5,1},{14,10},{10,6},{6,2},{15,11}... | collective-permute-start | bytes 3932168 | tf_op jit(solution)/shard_map/ppermute | solution.py:126
  1925.0 84.3 %collective-permute-start.80 = (bf16[2,128,2560]{2,1,0:T(8,128)(2,1)S(1)}, bf16[2,128,2560]{2,1,0:T(8,128)(2,1)S(1)}, u32[]{:S(2)}, u32[]{:S(2)}) collective-permute-start(bf16[2,128,2560]{2,1,0:T(8,128)(2,1)S(1)} %add.342), channel_id=1, source_target_pairs={{0,4},{4,8},{8,12},{1,5},{5,9},{9,13},{2,6},{6,10},{10,14},{3,7},{... | collective-permute-start | bytes 3932168 | tf_op jit(solution)/shard_map/ppermute | solution.py:125
  1954.3 81.4 %collective-permute-start.68 = (bf16[2,128,2560]{2,1,0:T(8,128)(2,1)S(1)}, bf16[2,128,2560]{2,1,0:T(8,128)(2,1)S(1)}, u32[]{:S(2)}, u32[]{:S(2)}) collective-permute-start(bf16[2,128,2560]{2,1,0:T(8,128)(2,1)S(1)} %add.334), channel_id=1, source_target_pairs={{0,4},{4,8},{8,12},{1,5},{5,9},{9,13},{2,6},{6,10},{10,14},{3,7},{... | collective-permute-start | bytes 3932168 | tf_op jit(solution)/shard_map/ppermute | solution.py:125
  1981.1 100.4 %collective-permute-start.46 = (bf16[8,128,640]{2,1,0:T(8,128)(2,1)S(1)}, bf16[8,128,640]{2,1,0:T(8,128)(2,1)S(1)}, u32[]{:S(2)}, u32[]{:S(2)}) collective-permute-start(bf16[8,128,640]{2,1,0:T(8,128)(2,1)S(1)} %pad_maximum_fusion.2), channel_id=1, source_target_pairs={{3,2},{7,6},{11,10},{15,14},{19,18},{23,22},{27,26},{31,30}} | collective-permute-start | bytes 3932168 | tf_op jit(solution)/shard_map/ppermute | solution.py:183
  2014.5 68.4 %collective-permute-start.45 = (bf16[8,128,640]{2,1,0:T(8,128)(2,1)S(1)}, bf16[8,128,640]{2,1,0:T(8,128)(2,1)S(1)}, u32[]{:S(2)}, u32[]{:S(2)}) collective-permute-start(bf16[8,128,640]{2,1,0:T(8,128)(2,1)S(1)} %pad_maximum_fusion.1), channel_id=1, source_target_pairs={{3,1},{7,5},{11,9},{15,13},{19,17},{23,21},{27,25},{31,29}} | collective-permute-start | bytes 3932168 | tf_op jit(solution)/shard_map/ppermute | solution.py:183
  (195 other events, 9396.6 us)

commit v2 on v1

--- a/solution.py
+++ b/solution.py
@@ -65,6 +65,28 @@
         cost_estimate=pl.CostEstimate(flops=40 * seqs * n * rows * width * 100, bytes_accessed=2 * (4 * n - 1) * seqs * rows * width, transcendentals=0),
         name="both_norms",
     )(rank, own, *from_left, *from_right, ln_rows)
+
+
+def up_kernel(pieces, m_ref, w_up_ref, g_ref):
+    rows = m_ref.shape[0] // pieces
+    for piece in range(pieces):
+        at = slice(piece * rows, (piece + 1) * rows)
+        wide = jnp.dot(m_ref[at, :], w_up_ref[...], preferred_element_type=jnp.float32)
+        g_ref[at, :] = (0.5 * wide * (1.0 + lax.erf(wide * 0.5**0.5))).astype(jnp.bfloat16)
+
+
+def up_and_gelu(m_norm, w_up, block=512, pieces=2):
+    tokens, width = m_norm.shape
+    return pl.pallas_call(
+        functools.partial(up_kernel, pieces),
+        grid=(w_up.shape[1] // block,),
+        in_specs=[pl.BlockSpec((tokens, width), lambda j: (0, 0)), pl.BlockSpec((width, block), lambda j: (0, j))],
+        out_specs=pl.BlockSpec((tokens, block), lambda j: (0, j)),
+        out_shape=jax.ShapeDtypeStruct((tokens, w_up.shape[1]), jnp.bfloat16),
+        compiler_params=pltpu.CompilerParams(vmem_limit_bytes=48 * 1024 * 1024),
+        cost_estimate=pl.CostEstimate(flops=2 * tokens * w_up.size, bytes_accessed=2 * (w_up.size + m_norm.size + tokens * w_up.shape[1]), transcendentals=tokens * w_up.shape[1]),
+        name="up_and_gelu",
+    )(m_norm, w_up)
 
 
 def down_kernel(n, rank_ref, o_ref, g_ref, w_out_ref, w_down_ref, *p_refs):
@@ -165,8 +187,7 @@
             a_norm, m_norm = both_norms(rank_arr, x_loc, from_left, from_right, ln_rows)
             a_norm, cos_here, sin_here, causal_here = lax.optimization_barrier((a_norm, cos_tab, sin_tab, causal))
             heads_out = attention_heads(a_norm, w_qkv[0], cos_here, sin_here, causal_here)
-            hidden = jnp.dot(m_norm.reshape(-1, width), w_up[0], preferred_element_type=jnp.float32)
-            hidden = jax.nn.gelu(hidden, approximate=False).astype(jnp.bfloat16)
+            hidden = up_and_gelu(m_norm.reshape(-1, width), w_up[0])
             *parts, first_send = out_and_down(rank_arr, n, seqs, heads_out.reshape(seqs * n * rows, -1), hidden, w_out[0], w_down[0])
             x_late, parts = lax.optimization_barrier((x_loc, parts))
             reduced = line_scatter(parts, first_send)

time: 2170 us -> 2030 us (0.935)
  matrix products: 570 us -> 251 us
  Pallas kernels: 296 us -> 443 us
  local copies, waits for them, and re-layouts: 61.5 us -> 96.2 us
    dot_general x8 -> x0, matrix products: 318 us -> none  [layer_here(): jnp.dot(m_norm.reshape(-1, width), w_up[0], preferred_element_type=jnp.fl...]
    pallas_call x0 -> x8, Pallas kernels: none -> 147 us  [up_and_gelu(): pl.pallas_call(functools.partial(up_kernel, pieces), grid=(w_up.shape[1]...]
    unnamed x276 -> x278, local copies, waits for them, and re-layouts: 3.63 us -> 38.4 us
  transfers between devices with their start and end apart: 105 -> 105, of which waited for: 48 -> 48; matrix products, arithmetic and copies ran while one was open for 28% -> 18% of each run, Pallas kernels for 10% -> 16%
where the time goes in v2:
time: 2030 us; the launch traced here: 2020 us
  waiting for transfers between devices  780 us (38%)
  Pallas kernels  443 us (22%)
  starting transfers between devices  268 us (13%)
  matrix products  251 us (12%)
  other arithmetic  174 us (9%)
  local copies, waits for them, and re-layouts  96.2 us (5%)
    ppermute x24, waiting for transfers between devices, line_gather(): lax.ppermute(from_right[-1], 'tp', [(z, z - 1) for z in range(1, n - step...  315 us
    pallas_call x8, Pallas kernels, out_and_down(): pl.pallas_call(functools.partial(down_kernel, n), grid_spec=pltpu.Prefetc...  190 us
    pallas_call x8, Pallas kernels, up_and_gelu(): pl.pallas_call(functools.partial(up_kernel, pieces), grid=(w_up.shape[1]...  147 us
    ppermute x8, waiting for transfers between devices, line_scatter(): rightward = lax.ppermute(send_right, 'tp', [(0, 1), (1, 2), (2, 3)])  133 us
    ppermute x8, waiting for transfers between devices, line_scatter(): rightward = lax.ppermute(middle, 'tp', [(0, 1), (1, 2)])  129 us
    dot_general x8, matrix products, attention_heads(): jnp.einsum('nsd,kjhd->nskjh', a_norm, w_qkv, preferred_element_type=jnp.f...  117 us
    ppermute x24, waiting for transfers between devices, line_gather(): lax.ppermute(from_left[-1], 'tp', [(z, z + 1) for z in range(step - 1, n...  115 us
    pallas_call x8, Pallas kernels, both_norms(): pl.pallas_call(functools.partial(norm_kernel, n), grid_spec=pltpu.Prefetc...  106 us
  transfers between devices with their start and end apart: 105, of which 48 were waited for; matrix products, arithmetic and copies ran while one was open for 18% of the time, Pallas kernels for 16%

profile of v2, /device:TPU:6, one launch (start us, length us, event | category | flops | bytes accessed | tf_op | source)
XLA Modules:
  0.0 2015.8 jit_solution(5172355552996147694)
XLA Ops:
  21.3 15.3 collective-permute-done.33.refs_1_
  44.5 20.1 collective-permute-done.22.refs_1_
  70.9 21.8 %collective-permute-done.11.refs_1_ = bf16[2,128,2560]{2,1,0:T(8,128)(2,1)} collective-permute-done((bf16[2,128,2560]{2,1,0:T(8,128)(2,1)S(1)}, bf16[2,128,2560]{2,1,0:T(8,128)(2,1)}, u32[]{:S(2)}, u32[]{:S(2)}) %collective-permute-start.11) | collective-permute-done | bytes 1310752 | tf_op jit(solution)/shard_map/ppermute | solution.py:136
  98.9 20.8 %collective-permute-done.refs_1_ = bf16[2,128,2560]{2,1,0:T(8,128)(2,1)S(1)} collective-permute-done((bf16[2,128,2560]{2,1,0:T(8,128)(2,1)S(1)}, bf16[2,128,2560]{2,1,0:T(8,128)(2,1)S(1)}, u32[]{:S(2)}, u32[]{:S(2)}) %collective-permute-start) | collective-permute-done | bytes 1310752 | tf_op jit(solution)/shard_map/ppermute | solution.py:136
  128.8 24.7 %collective-permute-done.37.refs_5_ = bf16[2,128,2560]{2,1,0:T(8,128)(2,1)} collective-permute-done((bf16[2,128,2560]{2,1,0:T(8,128)(2,1)S(1)}, bf16[2,128,2560]{2,1,0:T(8,128)(2,1)}, u32[]{:S(2)}, u32[]{:S(2)}) %collective-permute-start.37) | collective-permute-done | bytes 1310752 | tf_op jit(solution)/shard_map/ppermute | solution.py:137
  160.4 21.2 %collective-permute-done.26.refs_5_ = bf16[2,128,2560]{2,1,0:T(8,128)(2,1)} collective-permute-done((bf16[2,128,2560]{2,1,0:T(8,128)(2,1)}, bf16[2,128,2560]{2,1,0:T(8,128)(2,1)}, u32[]{:S(2)}, u32[]{:S(2)}) %collective-permute-start.26) | collective-permute-done | bytes 1310752 | tf_op jit(solution)/shard_map/ppermute | solution.py:137
  186.3 23.3 %collective-permute-done.38.refs_6_ = bf16[2,128,2560]{2,1,0:T(8,128)(2,1)} collective-permute-done((bf16[2,128,2560]{2,1,0:T(8,128)(2,1)}, bf16[2,128,2560]{2,1,0:T(8,128)(2,1)}, u32[]{:S(2)}, u32[]{:S(2)}) %collective-permute-start.38) | collective-permute-done | bytes 1310752 | tf_op jit(solution)/shard_map/ppermute | solution.py:137
  240.7 25.1 %collective-permute-done.4.refs_5_ = bf16[2,128,2560]{2,1,0:T(8,128)(2,1)} collective-permute-done((bf16[2,128,2560]{2,1,0:T(8,128)(2,1)}, bf16[2,128,2560]{2,1,0:T(8,128)(2,1)}, u32[]{:S(2)}, u32[]{:S(2)}) %collective-permute-start.4) | collective-permute-done | bytes 1310752 | tf_op jit(solution)/shard_map/ppermute | solution.py:137
  269.0 24.9 %collective-permute-done.27.refs_6_ = bf16[2,128,2560]{2,1,0:T(8,128)(2,1)} collective-permute-done((bf16[2,128,2560]{2,1,0:T(8,128)(2,1)}, bf16[2,128,2560]{2,1,0:T(8,128)(2,1)}, u32[]{:S(2)}, u32[]{:S(2)}) %collective-permute-start.27) | collective-permute-done | bytes 1310752 | tf_op jit(solution)/shard_map/ppermute | solution.py:137
  446.3 18.3 up_and_gelu.11.g_ref
  467.0 23.9 %out_and_down.11 = (bf16[2,128,2560]{2,1,0:T(8,128)(2,1)}, bf16[2,128,2560]{2,1,0:T(8,128)(2,1)}, bf16[2,128,2560]{2,1,0:T(8,128)(2,1)}, bf16[2,128,2560]{2,1,0:T(8,128)(2,1)}, bf16[2,128,2560]{2,1,0:T(8,128)(2,1)}) custom-call(s32[1]{0:T(128)} %bitcast.1.rank_ref, bf16[1024,640]{1,0:T(8,128)(2,1)} %reshape.524.o_ref, bf16[1024,2560]{1,0:T(8,128)(2,1)} %copy-done.3, ...), custom_call_target="tpu_custom_call" | custom-call | flops 16777216000 | bytes 28180480 | tf_op jit(solution)/shard_map/out_and_down/pallas_call | solution.py:113
  526.8 18.3 up_and_gelu.10.g_ref
  547.5 23.8 %out_and_down.10 = (bf16[2,128,2560]{2,1,0:T(8,128)(2,1)}, bf16[2,128,2560]{2,1,0:T(8,128)(2,1)}, bf16[2,128,2560]{2,1,0:T(8,128)(2,1)}, bf16[2,128,2560]{2,1,0:T(8,128)(2,1)}, bf16[2,128,2560]{2,1,0:T(8,128)(2,1)}) custom-call(s32[1]{0:T(128)} %bitcast.1.rank_ref, bf16[1024,640]{1,0:T(8,128)(2,1)} %reshape.523.o_ref, bf16[1024,2560]{1,0:T(8,128)(2,1)} %copy-done.4, ...), custom_call_target="tpu_custom_call" | custom-call | flops 16777216000 | bytes 28180480 | tf_op jit(solution)/shard_map/out_and_down/pallas_call | solution.py:113
  606.9 18.4 up_and_gelu.9.g_ref
  627.6 23.8 %out_and_down.9 = (bf16[2,128,2560]{2,1,0:T(8,128)(2,1)}, bf16[2,128,2560]{2,1,0:T(8,128)(2,1)}, bf16[2,128,2560]{2,1,0:T(8,128)(2,1)}, bf16[2,128,2560]{2,1,0:T(8,128)(2,1)}, bf16[2,128,2560]{2,1,0:T(8,128)(2,1)}) custom-call(s32[1]{0:T(128)} %bitcast.1.rank_ref, bf16[1024,640]{1,0:T(8,128)(2,1)} %reshape.522.o_ref, bf16[1024,2560]{1,0:T(8,128)(2,1)} %copy-done.5, ...), custom_call_target="tpu_custom_call" | custom-call | flops 16777216000 | bytes 28180480 | tf_op jit(solution)/shard_map/out_and_down/pallas_call | solution.py:113
  684.6 18.3 up_and_gelu.8.g_ref
  705.4 23.7 %out_and_down.8 = (bf16[2,128,2560]{2,1,0:T(8,128)(2,1)}, bf16[2,128,2560]{2,1,0:T(8,128)(2,1)}, bf16[2,128,2560]{2,1,0:T(8,128)(2,1)}, bf16[2,128,2560]{2,1,0:T(8,128)(2,1)}, bf16[2,128,2560]{2,1,0:T(8,128)(2,1)}) custom-call(s32[1]{0:T(128)} %bitcast.1.rank_ref, bf16[1024,640]{1,0:T(8,128)(2,1)} %reshape.521.o_ref, bf16[1024,2560]{1,0:T(8,128)(2,1)} %copy-done.6, ...), custom_call_target="tpu_custom_call" | custom-call | flops 16777216000 | bytes 28180480 | tf_op jit(solution)/shard_map/out_and_down/pallas_call | solution.py:113
  742.8 17.0 collective-permute-done.6
  767.0 20.8 %collective-permute-done.40 = bf16[2,128,2560]{2,1,0:T(8,128)(2,1)S(1)} collective-permute-done((bf16[2,128,2560]{2,1,0:T(8,128)(2,1)S(1)}, bf16[2,128,2560]{2,1,0:T(8,128)(2,1)S(1)}, u32[]{:S(2)}, u32[]{:S(2)}) %collective-permute-start.40) | collective-permute-done | bytes 1310752 | tf_op jit(solution)/shard_map/ppermute | solution.py:144
  800.7 15.2 collective-permute-done.29
  875.0 17.1 collective-permute-start.19
  912.5 15.8 collective-permute-done.30
  932.8 23.5 %collective-permute-done.19 = bf16[2,128,2560]{2,1,0:T(8,128)(2,1)S(1)} collective-permute-done((bf16[2,128,2560]{2,1,0:T(8,128)(2,1)S(1)}, bf16[2,128,2560]{2,1,0:T(8,128)(2,1)S(1)}, u32[]{:S(2)}, u32[]{:S(2)}) %collective-permute-start.19) | collective-permute-done | bytes 1310752 | tf_op jit(solution)/shard_map/ppermute | solution.py:147
  965.2 19.2 collective-permute-done.8
  992.6 19.9 collective-permute-done.87.refs_1_
  1023.7 17.0 collective-permute-done.72.refs_1_
  1049.4 26.7 %collective-permute-done.75.refs_4_ = bf16[2,128,2560]{2,1,0:T(8,128)(2,1)} collective-permute-done((bf16[2,128,2560]{2,1,0:T(8,128)(2,1)S(1)}, bf16[2,128,2560]{2,1,0:T(8,128)(2,1)}, u32[]{:S(2)}, u32[]{:S(2)}) %collective-permute-start.75) | collective-permute-done | bytes 1310752 | tf_op jit(solution)/shard_map/ppermute | solution.py:137
  1081.4 22.7 %collective-permute-done.63.refs_4_ = bf16[2,128,2560]{2,1,0:T(8,128)(2,1)S(1)} collective-permute-done((bf16[2,128,2560]{2,1,0:T(8,128)(2,1)S(1)}, bf16[2,128,2560]{2,1,0:T(8,128)(2,1)S(1)}, u32[]{:S(2)}, u32[]{:S(2)}) %collective-permute-start.63) | collective-permute-done | bytes 1310752 | tf_op jit(solution)/shard_map/ppermute | solution.py:137
  1113.5 18.7 collective-permute-done.92.refs_6_
  1163.4 25.1 %collective-permute-done.76.refs_5_ = bf16[2,128,2560]{2,1,0:T(8,128)(2,1)} collective-permute-done((bf16[2,128,2560]{2,1,0:T(8,128)(2,1)}, bf16[2,128,2560]{2,1,0:T(8,128)(2,1)}, u32[]{:S(2)}, u32[]{:S(2)}) %collective-permute-start.76) | collective-permute-done | bytes 1310752 | tf_op jit(solution)/shard_map/ppermute | solution.py:137
  1190.5 16.0 fusion.91
  1219.6 25.1 %collective-permute-done.52.refs_5_ = bf16[2,128,2560]{2,1,0:T(8,128)(2,1)} collective-permute-done((bf16[2,128,2560]{2,1,0:T(8,128)(2,1)}, bf16[2,128,2560]{2,1,0:T(8,128)(2,1)}, u32[]{:S(2)}, u32[]{:S(2)}) %collective-permute-start.52) | collective-permute-done | bytes 1310752 | tf_op jit(solution)/shard_map/ppermute | solution.py:137
  1247.9 24.8 %collective-permute-done.77.refs_6_ = bf16[2,128,2560]{2,1,0:T(8,128)(2,1)} collective-permute-done((bf16[2,128,2560]{2,1,0:T(8,128)(2,1)}, bf16[2,128,2560]{2,1,0:T(8,128)(2,1)}, u32[]{:S(2)}, u32[]{:S(2)}) %collective-permute-start.77) | collective-permute-done | bytes 1310752 | tf_op jit(solution)/shard_map/ppermute | solution.py:137
  1410.2 18.3 up_and_gelu.15.g_ref
  1430.9 23.8 %out_and_down.15 = (bf16[2,128,2560]{2,1,0:T(8,128)(2,1)}, bf16[2,128,2560]{2,1,0:T(8,128)(2,1)}, bf16[2,128,2560]{2,1,0:T(8,128)(2,1)}, bf16[2,128,2560]{2,1,0:T(8,128)(2,1)}, bf16[2,128,2560]{2,1,0:T(8,128)(2,1)}) custom-call(s32[1]{0:T(128)} %bitcast.1.rank_ref, bf16[1024,640]{1,0:T(8,128)(2,1)} %reshape.528.o_ref, bf16[1024,2560]{1,0:T(8,128)(2,1)} %copy-done.7, ...), custom_call_target="tpu_custom_call" | custom-call | flops 16777216000 | bytes 28180480 | tf_op jit(solution)/shard_map/out_and_down/pallas_call | solution.py:113
  1490.5 18.3 up_and_gelu.14.g_ref
  1511.2 23.8 %out_and_down.14 = (bf16[2,128,2560]{2,1,0:T(8,128)(2,1)}, bf16[2,128,2560]{2,1,0:T(8,128)(2,1)}, bf16[2,128,2560]{2,1,0:T(8,128)(2,1)}, bf16[2,128,2560]{2,1,0:T(8,128)(2,1)}, bf16[2,128,2560]{2,1,0:T(8,128)(2,1)}) custom-call(s32[1]{0:T(128)} %bitcast.1.rank_ref, bf16[1024,640]{1,0:T(8,128)(2,1)} %reshape.527.o_ref, bf16[1024,2560]{1,0:T(8,128)(2,1)} %copy-done.8, ...), custom_call_target="tpu_custom_call" | custom-call | flops 16777216000 | bytes 28180480 | tf_op jit(solution)/shard_map/out_and_down/pallas_call | solution.py:113
  1570.5 18.3 up_and_gelu.13.g_ref
  1591.2 23.8 %out_and_down.13 = (bf16[2,128,2560]{2,1,0:T(8,128)(2,1)}, bf16[2,128,2560]{2,1,0:T(8,128)(2,1)}, bf16[2,128,2560]{2,1,0:T(8,128)(2,1)}, bf16[2,128,2560]{2,1,0:T(8,128)(2,1)}, bf16[2,128,2560]{2,1,0:T(8,128)(2,1)}) custom-call(s32[1]{0:T(128)} %bitcast.1.rank_ref, bf16[1024,640]{1,0:T(8,128)(2,1)} %reshape.526.o_ref, bf16[1024,2560]{1,0:T(8,128)(2,1)} %copy-done.9, ...), custom_call_target="tpu_custom_call" | custom-call | flops 16777216000 | bytes 28180480 | tf_op jit(solution)/shard_map/out_and_down/pallas_call | solution.py:113
  1648.2 18.4 up_and_gelu.12.g_ref
  1669.0 23.8 %out_and_down.12 = (bf16[2,128,2560]{2,1,0:T(8,128)(2,1)}, bf16[2,128,2560]{2,1,0:T(8,128)(2,1)}, bf16[2,128,2560]{2,1,0:T(8,128)(2,1)}, bf16[2,128,2560]{2,1,0:T(8,128)(2,1)}, bf16[2,128,2560]{2,1,0:T(8,128)(2,1)}) custom-call(s32[1]{0:T(128)} %bitcast.1.rank_ref, bf16[1024,640]{1,0:T(8,128)(2,1)} %reshape.525.o_ref, bf16[1024,2560]{1,0:T(8,128)(2,1)} %copy-done.2, ...), custom_call_target="tpu_custom_call" | custom-call | flops 16777216000 | bytes 28180480 | tf_op jit(solution)/shard_map/out_and_down/pallas_call | solution.py:113
  1703.7 19.8 collective-permute-done.54
  1730.3 21.2 %collective-permute-done.79 = bf16[2,128,2560]{2,1,0:T(8,128)(2,1)S(1)} collective-permute-done((bf16[2,128,2560]{2,1,0:T(8,128)(2,1)S(1)}, bf16[2,128,2560]{2,1,0:T(8,128)(2,1)S(1)}, u32[]{:S(2)}, u32[]{:S(2)}) %collective-permute-start.79) | collective-permute-done | bytes 1310752 | tf_op jit(solution)/shard_map/ppermute | solution.py:144
  1759.4 20.2 %collective-permute-done.67 = bf16[2,128,2560]{2,1,0:T(8,128)(2,1)S(1)} collective-permute-done((bf16[2,128,2560]{2,1,0:T(8,128)(2,1)S(1)}, bf16[2,128,2560]{2,1,0:T(8,128)(2,1)S(1)}, u32[]{:S(2)}, u32[]{:S(2)}) %collective-permute-start.67) | collective-permute-done | bytes 1310752 | tf_op jit(solution)/shard_map/ppermute | solution.py:144
  1818.6 17.2 collective-permute-done.55
  1838.7 25.2 %collective-permute-done.80 = bf16[2,128,2560]{2,1,0:T(8,128)(2,1)S(1)} collective-permute-done((bf16[2,128,2560]{2,1,0:T(8,128)(2,1)S(1)}, bf16[2,128,2560]{2,1,0:T(8,128)(2,1)S(1)}, u32[]{:S(2)}, u32[]{:S(2)}) %collective-permute-start.80) | collective-permute-done | bytes 1310752 | tf_op jit(solution)/shard_map/ppermute | solution.py:147
  1870.1 20.2 %collective-permute-done.68 = bf16[2,128,2560]{2,1,0:T(8,128)(2,1)S(1)} collective-permute-done((bf16[2,128,2560]{2,1,0:T(8,128)(2,1)S(1)}, bf16[2,128,2560]{2,1,0:T(8,128)(2,1)S(1)}, u32[]{:S(2)}, u32[]{:S(2)}) %collective-permute-start.68) | collective-permute-done | bytes 1310752 | tf_op jit(solution)/shard_map/ppermute | solution.py:147
  1893.3 15.1 collective-permute-done.56
  (611 shorter events, 1014.6 us)
Async XLA Ops:
  15.7 77.0 %collective-permute-start.11 = (bf16[2,128,2560]{2,1,0:T(8,128)(2,1)S(1)}, bf16[2,128,2560]{2,1,0:T(8,128)(2,1)}, u32[]{:S(2)}, u32[]{:S(2)}) collective-permute-start(bf16[2,128,2560]{2,1,0:T(8,128)(2,1)S(1)} %get-tuple-element.165.refs_0_), channel_id=1, source_target_pairs={{0,4},{4,8},{8,12},{1,5},{5,9},{9,13},{2,6},{6,10},{10,14},{3,7},{... | collective-permute-start | bytes 3932168 | tf_op jit(solution)/shard_map/ppermute | solution.py:136
  41.0 78.7 %collective-permute-start = (bf16[2,128,2560]{2,1,0:T(8,128)(2,1)S(1)}, bf16[2,128,2560]{2,1,0:T(8,128)(2,1)S(1)}, u32[]{:S(2)}, u32[]{:S(2)}) collective-permute-start(bf16[2,128,2560]{2,1,0:T(8,128)(2,1)S(1)} %get-tuple-element.149.refs_0_), channel_id=1, source_target_pairs={{0,4},{4,8},{8,12},{1,5},{5,9},{9,13},{2,6},{6,10},{10,14},{3,7},{... | collective-permute-start | bytes 3932168 | tf_op jit(solution)/shard_map/ppermute | solution.py:136
  97.2 61.9 %collective-permute-start.23 = (bf16[2,128,2560]{2,1,0:T(8,128)(2,1)}, bf16[2,128,2560]{2,1,0:T(8,128)(2,1)}, u32[]{:S(2)}, u32[]{:S(2)}) collective-permute-start(bf16[2,128,2560]{2,1,0:T(8,128)(2,1)} %collective-permute-done.22.refs_1_), channel_id=1, source_target_pairs={{4,8},{8,12},{5,9},{9,13},{6,10},{10,14},{7,11},{11,15},{20,24},{2... | collective-permute-start | bytes 3932168 | tf_op jit(solution)/shard_map/ppermute | solution.py:136
  119.7 61.9 %collective-permute-start.26 = (bf16[2,128,2560]{2,1,0:T(8,128)(2,1)}, bf16[2,128,2560]{2,1,0:T(8,128)(2,1)}, u32[]{:S(2)}, u32[]{:S(2)}) collective-permute-start(bf16[2,128,2560]{2,1,0:T(8,128)(2,1)} %collective-permute-done.25.refs_4_), channel_id=1, source_target_pairs={{4,0},{8,4},{5,1},{9,5},{6,2},{10,6},{7,3},{11,7},{20,16},{24,20},... | collective-permute-start | bytes 3932168 | tf_op jit(solution)/shard_map/ppermute | solution.py:137
  159.1 78.7 %collective-permute-start.15 = (bf16[2,128,2560]{2,1,0:T(8,128)(2,1)}, bf16[2,128,2560]{2,1,0:T(8,128)(2,1)}, u32[]{:S(2)}, u32[]{:S(2)}) collective-permute-start(bf16[2,128,2560]{2,1,0:T(8,128)(2,1)} %copy-done.126), channel_id=1, source_target_pairs={{4,0},{8,4},{5,1},{9,5},{6,2},{10,6},{7,3},{11,7},{20,16},{24,20},... | collective-permute-start | bytes 3932168 | tf_op jit(solution)/shard_map/ppermute | solution.py:137
  183.3 82.5 %collective-permute-start.4 = (bf16[2,128,2560]{2,1,0:T(8,128)(2,1)}, bf16[2,128,2560]{2,1,0:T(8,128)(2,1)}, u32[]{:S(2)}, u32[]{:S(2)}) collective-permute-start(bf16[2,128,2560]{2,1,0:T(8,128)(2,1)} %copy-done.125), channel_id=1, source_target_pairs={{4,0},{8,4},{5,1},{9,5},{6,2},{10,6},{7,3},{11,7},{20,16},{24,20},... | collective-permute-start | bytes 3932168 | tf_op jit(solution)/shard_map/ppermute | solution.py:137
  184.6 83.0 %collective-permute-start.24 = (bf16[2,128,2560]{2,1,0:T(8,128)(2,1)}, bf16[2,128,2560]{2,1,0:T(8,128)(2,1)}, u32[]{:S(2)}, u32[]{:S(2)}) collective-permute-start(bf16[2,128,2560]{2,1,0:T(8,128)(2,1)} %collective-permute-done.23.refs_2_), channel_id=1, source_target_pairs={{8,12},{9,13},{10,14},{11,15},{24,28},{25,29},{26,30},{27,31}} | collective-permute-start | bytes 3932168 | tf_op jit(solution)/shard_map/ppermute | solution.py:136
  209.7 84.3 %collective-permute-start.27 = (bf16[2,128,2560]{2,1,0:T(8,128)(2,1)}, bf16[2,128,2560]{2,1,0:T(8,128)(2,1)}, u32[]{:S(2)}, u32[]{:S(2)}) collective-permute-start(bf16[2,128,2560]{2,1,0:T(8,128)(2,1)} %collective-permute-done.26.refs_5_), channel_id=1, source_target_pairs={{4,0},{5,1},{6,2},{7,3},{20,16},{21,17},{22,18},{23,19}} | collective-permute-start | bytes 3932168 | tf_op jit(solution)/shard_map/ppermute | solution.py:137
  237.7 106.7 %collective-permute-start.13 = (bf16[2,128,2560]{2,1,0:T(8,128)(2,1)}, bf16[2,128,2560]{2,1,0:T(8,128)(2,1)}, u32[]{:S(2)}, u32[]{:S(2)}) collective-permute-start(bf16[2,128,2560]{2,1,0:T(8,128)(2,1)} %collective-permute-done.12.refs_2_), channel_id=1, source_target_pairs={{8,12},{9,13},{10,14},{11,15},{24,28},{25,29},{26,30},{27,31}} | collective-permute-start | bytes 3932168 | tf_op jit(solution)/shard_map/ppermute | solution.py:136
  239.5 105.0 %collective-permute-start.16 = (bf16[2,128,2560]{2,1,0:T(8,128)(2,1)}, bf16[2,128,2560]{2,1,0:T(8,128)(2,1)}, u32[]{:S(2)}, u32[]{:S(2)}) collective-permute-start(bf16[2,128,2560]{2,1,0:T(8,128)(2,1)} %collective-permute-done.15.refs_5_), channel_id=1, source_target_pairs={{4,0},{5,1},{6,2},{7,3},{20,16},{21,17},{22,18},{23,19}} | collective-permute-start | bytes 3932168 | tf_op jit(solution)/shard_map/ppermute | solution.py:137
  265.8 114.1 %collective-permute-start.2 = (bf16[2,128,2560]{2,1,0:T(8,128)(2,1)}, bf16[2,128,2560]{2,1,0:T(8,128)(2,1)}, u32[]{:S(2)}, u32[]{:S(2)}) collective-permute-start(bf16[2,128,2560]{2,1,0:T(8,128)(2,1)} %collective-permute-done.1.refs_2_), channel_id=1, source_target_pairs={{8,12},{9,13},{10,14},{11,15},{24,28},{25,29},{26,30},{27,31}} | collective-permute-start | bytes 3932168 | tf_op jit(solution)/shard_map/ppermute | solution.py:136
  267.5 112.4 %collective-permute-start.5 = (bf16[2,128,2560]{2,1,0:T(8,128)(2,1)}, bf16[2,128,2560]{2,1,0:T(8,128)(2,1)}, u32[]{:S(2)}, u32[]{:S(2)}) collective-permute-start(bf16[2,128,2560]{2,1,0:T(8,128)(2,1)} %collective-permute-done.4.refs_5_), channel_id=1, source_target_pairs={{4,0},{5,1},{6,2},{7,3},{20,16},{21,17},{22,18},{23,19}} | collective-permute-start | bytes 3932168 | tf_op jit(solution)/shard_map/ppermute | solution.py:137
  490.9 239.6 %collective-permute-start.39 = (bf16[2,128,2560]{2,1,0:T(8,128)(2,1)}, bf16[2,128,2560]{2,1,0:T(8,128)(2,1)}, u32[]{:S(2)}, u32[]{:S(2)}) collective-permute-start(bf16[2,128,2560]{2,1,0:T(8,128)(2,1)} %get-tuple-element.201), channel_id=1, source_target_pairs={{0,4},{12,8},{1,5},{13,9},{2,6},{14,10},{3,7},{15,11},{16,20},{28,... | collective-permute-start | bytes 3932168 | tf_op jit(solution)/shard_map/ppermute | solution.py:142
  571.3 163.5 %collective-permute-start.28 = (bf16[2,128,2560]{2,1,0:T(8,128)(2,1)}, bf16[2,128,2560]{2,1,0:T(8,128)(2,1)}, u32[]{:S(2)}, u32[]{:S(2)}) collective-permute-start(bf16[2,128,2560]{2,1,0:T(8,128)(2,1)} %get-tuple-element.185), channel_id=1, source_target_pairs={{0,4},{12,8},{1,5},{13,9},{2,6},{14,10},{3,7},{15,11},{16,20},{28,... | collective-permute-start | bytes 3932168 | tf_op jit(solution)/shard_map/ppermute | solution.py:142
  651.4 86.2 %collective-permute-start.17 = (bf16[2,128,2560]{2,1,0:T(8,128)(2,1)}, bf16[2,128,2560]{2,1,0:T(8,128)(2,1)}, u32[]{:S(2)}, u32[]{:S(2)}) collective-permute-start(bf16[2,128,2560]{2,1,0:T(8,128)(2,1)} %get-tuple-element.169), channel_id=1, source_target_pairs={{0,4},{12,8},{1,5},{13,9},{2,6},{14,10},{3,7},{15,11},{16,20},{28,... | collective-permute-start | bytes 3932168 | tf_op jit(solution)/shard_map/ppermute | solution.py:142
  737.6 78.3 %collective-permute-start.29 = (bf16[2,128,2560]{2,1,0:T(8,128)(2,1)S(1)}, bf16[2,128,2560]{2,1,0:T(8,128)(2,1)S(1)}, u32[]{:S(2)}, u32[]{:S(2)}) collective-permute-start(bf16[2,128,2560]{2,1,0:T(8,128)(2,1)S(1)} %add.306), channel_id=1, source_target_pairs={{0,4},{4,8},{1,5},{5,9},{2,6},{6,10},{3,7},{7,11},{16,20},{20,24},... | collective-permute-start | bytes 3932168 | tf_op jit(solution)/shard_map/ppermute | solution.py:144
  762.0 82.1 %collective-permute-start.18 = (bf16[2,128,2560]{2,1,0:T(8,128)(2,1)}, bf16[2,128,2560]{2,1,0:T(8,128)(2,1)}, u32[]{:S(2)}, u32[]{:S(2)}) collective-permute-start(bf16[2,128,2560]{2,1,0:T(8,128)(2,1)} %add.298), channel_id=1, source_target_pairs={{0,4},{4,8},{1,5},{5,9},{2,6},{6,10},{3,7},{7,11},{16,20},{20,24},... | collective-permute-start | bytes 3932168 | tf_op jit(solution)/shard_map/ppermute | solution.py:144
  790.9 81.2 %collective-permute-start.7 = (bf16[2,128,2560]{2,1,0:T(8,128)(2,1)S(1)}, bf16[2,128,2560]{2,1,0:T(8,128)(2,1)}, u32[]{:S(2)}, u32[]{:S(2)}) collective-permute-start(bf16[2,128,2560]{2,1,0:T(8,128)(2,1)S(1)} %add.290), channel_id=1, source_target_pairs={{0,4},{4,8},{1,5},{5,9},{2,6},{6,10},{3,7},{7,11},{16,20},{20,24},... | collective-permute-start | bytes 3932168 | tf_op jit(solution)/shard_map/ppermute | solution.py:144
  818.2 82.0 %collective-permute-start.41 = (bf16[2,128,2560]{2,1,0:T(8,128)(2,1)}, bf16[2,128,2560]{2,1,0:T(8,128)(2,1)}, u32[]{:S(2)}, u32[]{:S(2)}) collective-permute-start(bf16[2,128,2560]{2,1,0:T(8,128)(2,1)} %add.315), channel_id=1, source_target_pairs={{0,4},{4,8},{8,12},{1,5},{5,9},{9,13},{2,6},{6,10},{10,14},{3,7},{... | collective-permute-start | bytes 3932168 | tf_op jit(solution)/shard_map/ppermute | solution.py:147
  845.4 82.9 %collective-permute-start.30 = (bf16[2,128,2560]{2,1,0:T(8,128)(2,1)S(1)}, bf16[2,128,2560]{2,1,0:T(8,128)(2,1)S(1)}, u32[]{:S(2)}, u32[]{:S(2)}) collective-permute-start(bf16[2,128,2560]{2,1,0:T(8,128)(2,1)S(1)} %add.307), channel_id=1, source_target_pairs={{0,4},{4,8},{8,12},{1,5},{5,9},{9,13},{2,6},{6,10},{10,14},{3,7},{... | collective-permute-start | bytes 3932168 | tf_op jit(solution)/shard_map/ppermute | solution.py:147
  875.0 81.3 %collective-permute-start.19 = (bf16[2,128,2560]{2,1,0:T(8,128)(2,1)S(1)}, bf16[2,128,2560]{2,1,0:T(8,128)(2,1)S(1)}, u32[]{:S(2)}, u32[]{:S(2)}) collective-permute-start(bf16[2,128,2560]{2,1,0:T(8,128)(2,1)S(1)} %add.299), channel_id=1, source_target_pairs={{0,4},{4,8},{8,12},{1,5},{5,9},{9,13},{2,6},{6,10},{10,14},{3,7},{... | collective-permute-start | bytes 3932168 | tf_op jit(solution)/shard_map/ppermute | solution.py:147
  900.3 63.6 %collective-permute-start.10 = (bf16[2,128,2560]{2,1,0:T(8,128)(2,1)S(1)}, bf16[2,128,2560]{2,1,0:T(8,128)(2,1)S(1)}, u32[]{:S(2)}, u32[]{:S(2)}) collective-permute-start(bf16[2,128,2560]{2,1,0:T(8,128)(2,1)S(1)} %add.293), channel_id=1, source_target_pairs={{12,8},{8,4},{4,0},{13,9},{9,5},{5,1},{14,10},{10,6},{6,2},{15,11}... | collective-permute-start | bytes 3932168 | tf_op jit(solution)/shard_map/ppermute | solution.py:148
  904.0 80.5 %collective-permute-start.8 = (bf16[2,128,2560]{2,1,0:T(8,128)(2,1)S(1)}, bf16[2,128,2560]{2,1,0:T(8,128)(2,1)S(1)}, u32[]{:S(2)}, u32[]{:S(2)}) collective-permute-start(bf16[2,128,2560]{2,1,0:T(8,128)(2,1)S(1)} %add.291), channel_id=1, source_target_pairs={{0,4},{4,8},{8,12},{1,5},{5,9},{9,13},{2,6},{6,10},{10,14},{3,7},{... | collective-permute-start | bytes 3932168 | tf_op jit(solution)/shard_map/ppermute | solution.py:147
  1014.6 61.5 %collective-permute-start.75 = (bf16[2,128,2560]{2,1,0:T(8,128)(2,1)S(1)}, bf16[2,128,2560]{2,1,0:T(8,128)(2,1)}, u32[]{:S(2)}, u32[]{:S(2)}) collective-permute-start(bf16[2,128,2560]{2,1,0:T(8,128)(2,1)S(1)} %broadcast_select_fusion.1.refs_0_), channel_id=1, source_target_pairs={{4,0},{8,4},{12,8},{5,1},{9,5},{13,9},{6,2},{10,6},{14,10},{7,3},{... | collective-permute-start | bytes 3932168 | tf_op jit(solution)/shard_map/ppermute | solution.py:137
  1016.3 63.9 %collective-permute-start.60 = (bf16[2,128,2560]{2,1,0:T(8,128)(2,1)S(1)}, bf16[2,128,2560]{2,1,0:T(8,128)(2,1)}, u32[]{:S(2)}, u32[]{:S(2)}) collective-permute-start(bf16[2,128,2560]{2,1,0:T(8,128)(2,1)S(1)} %broadcast_select_fusion.2.refs_0_), channel_id=1, source_target_pairs={{0,4},{4,8},{8,12},{1,5},{5,9},{9,13},{2,6},{6,10},{10,14},{3,7},{... | collective-permute-start | bytes 3932168 | tf_op jit(solution)/shard_map/ppermute | solution.py:136
  1040.6 63.5 %collective-permute-start.63 = (bf16[2,128,2560]{2,1,0:T(8,128)(2,1)S(1)}, bf16[2,128,2560]{2,1,0:T(8,128)(2,1)S(1)}, u32[]{:S(2)}, u32[]{:S(2)}) collective-permute-start(bf16[2,128,2560]{2,1,0:T(8,128)(2,1)S(1)} %broadcast_select_fusion.2.refs_0_), channel_id=1, source_target_pairs={{4,0},{8,4},{12,8},{5,1},{9,5},{13,9},{6,2},{10,6},{14,10},{7,3},{... | collective-permute-start | bytes 3932168 | tf_op jit(solution)/shard_map/ppermute | solution.py:137
  1041.9 65.0 %collective-permute-start.89 = (bf16[2,128,2560]{2,1,0:T(8,128)(2,1)S(1)}, bf16[2,128,2560]{2,1,0:T(8,128)(2,1)S(1)}, u32[]{:S(2)}, u32[]{:S(2)}) collective-permute-start(bf16[2,128,2560]{2,1,0:T(8,128)(2,1)S(1)} %collective-permute-done.88.refs_2_), channel_id=1, source_target_pairs={{8,12},{9,13},{10,14},{11,15},{24,28},{25,29},{26,30},{27,31}} | collective-permute-start | bytes 3932168 | tf_op jit(solution)/shard_map/ppermute | solution.py:136
  1047.9 84.3 %collective-permute-start.92 = (bf16[2,128,2560]{2,1,0:T(8,128)(2,1)S(1)}, bf16[2,128,2560]{2,1,0:T(8,128)(2,1)S(1)}, u32[]{:S(2)}, u32[]{:S(2)}) collective-permute-start(bf16[2,128,2560]{2,1,0:T(8,128)(2,1)S(1)} %collective-permute-done.91.refs_5_), channel_id=1, source_target_pairs={{4,0},{5,1},{6,2},{7,3},{20,16},{21,17},{22,18},{23,19}} | collective-permute-start | bytes 3932168 | tf_op jit(solution)/shard_map/ppermute | solution.py:137
  1076.1 72.0 %collective-permute-start.48 = (bf16[2,128,2560]{2,1,0:T(8,128)(2,1)S(1)}, bf16[2,128,2560]{2,1,0:T(8,128)(2,1)S(1)}, u32[]{:S(2)}, u32[]{:S(2)}) collective-permute-start(bf16[2,128,2560]{2,1,0:T(8,128)(2,1)S(1)} %broadcast_select_fusion.3.refs_0_), channel_id=1, source_target_pairs={{0,4},{4,8},{8,12},{1,5},{5,9},{9,13},{2,6},{6,10},{10,14},{3,7},{... | collective-permute-start | bytes 3932168 | tf_op jit(solution)/shard_map/ppermute | solution.py:136
  1080.1 80.3 %collective-permute-start.51 = (bf16[2,128,2560]{2,1,0:T(8,128)(2,1)S(1)}, bf16[2,128,2560]{2,1,0:T(8,128)(2,1)}, u32[]{:S(2)}, u32[]{:S(2)}) collective-permute-start(bf16[2,128,2560]{2,1,0:T(8,128)(2,1)S(1)} %broadcast_select_fusion.3.refs_0_), channel_id=1, source_target_pairs={{4,0},{8,4},{12,8},{5,1},{9,5},{13,9},{6,2},{10,6},{14,10},{7,3},{... | collective-permute-start | bytes 3932168 | tf_op jit(solution)/shard_map/ppermute | solution.py:137
  1106.9 81.6 %collective-permute-start.76 = (bf16[2,128,2560]{2,1,0:T(8,128)(2,1)}, bf16[2,128,2560]{2,1,0:T(8,128)(2,1)}, u32[]{:S(2)}, u32[]{:S(2)}) collective-permute-start(bf16[2,128,2560]{2,1,0:T(8,128)(2,1)} %collective-permute-done.75.refs_4_), channel_id=1, source_target_pairs={{4,0},{8,4},{5,1},{9,5},{6,2},{10,6},{7,3},{11,7},{20,16},{24,20},... | collective-permute-start | bytes 3932168 | tf_op jit(solution)/shard_map/ppermute | solution.py:137
  1148.1 68.4 %collective-permute-start.64 = (bf16[2,128,2560]{2,1,0:T(8,128)(2,1)}, bf16[2,128,2560]{2,1,0:T(8,128)(2,1)}, u32[]{:S(2)}, u32[]{:S(2)}) collective-permute-start(bf16[2,128,2560]{2,1,0:T(8,128)(2,1)} %copy-done.128), channel_id=1, source_target_pairs={{4,0},{8,4},{5,1},{9,5},{6,2},{10,6},{7,3},{11,7},{20,16},{24,20},... | collective-permute-start | bytes 3932168 | tf_op jit(solution)/shard_map/ppermute | solution.py:137
  1162.1 82.6 %collective-permute-start.52 = (bf16[2,128,2560]{2,1,0:T(8,128)(2,1)}, bf16[2,128,2560]{2,1,0:T(8,128)(2,1)}, u32[]{:S(2)}, u32[]{:S(2)}) collective-permute-start(bf16[2,128,2560]{2,1,0:T(8,128)(2,1)} %collective-permute-done.51.refs_4_), channel_id=1, source_target_pairs={{4,0},{8,4},{5,1},{9,5},{6,2},{10,6},{7,3},{11,7},{20,16},{24,20},... | collective-permute-start | bytes 3932168 | tf_op jit(solution)/shard_map/ppermute | solution.py:137
  1189.2 83.5 %collective-permute-start.77 = (bf16[2,128,2560]{2,1,0:T(8,128)(2,1)}, bf16[2,128,2560]{2,1,0:T(8,128)(2,1)}, u32[]{:S(2)}, u32[]{:S(2)}) collective-permute-start(bf16[2,128,2560]{2,1,0:T(8,128)(2,1)} %collective-permute-done.76.refs_5_), channel_id=1, source_target_pairs={{4,0},{5,1},{6,2},{7,3},{20,16},{21,17},{22,18},{23,19}} | collective-permute-start | bytes 3932168 | tf_op jit(solution)/shard_map/ppermute | solution.py:137
  1216.6 92.2 %collective-permute-start.62 = (bf16[2,128,2560]{2,1,0:T(8,128)(2,1)}, bf16[2,128,2560]{2,1,0:T(8,128)(2,1)}, u32[]{:S(2)}, u32[]{:S(2)}) collective-permute-start(bf16[2,128,2560]{2,1,0:T(8,128)(2,1)} %collective-permute-done.61.refs_2_), channel_id=1, source_target_pairs={{8,12},{9,13},{10,14},{11,15},{24,28},{25,29},{26,30},{27,31}} | collective-permute-start | bytes 3932168 | tf_op jit(solution)/shard_map/ppermute | solution.py:136
  1218.3 90.5 %collective-permute-start.65 = (bf16[2,128,2560]{2,1,0:T(8,128)(2,1)}, bf16[2,128,2560]{2,1,0:T(8,128)(2,1)}, u32[]{:S(2)}, u32[]{:S(2)}) collective-permute-start(bf16[2,128,2560]{2,1,0:T(8,128)(2,1)} %collective-permute-done.64.refs_5_), channel_id=1, source_target_pairs={{4,0},{5,1},{6,2},{7,3},{20,16},{21,17},{22,18},{23,19}} | collective-permute-start | bytes 3932168 | tf_op jit(solution)/shard_map/ppermute | solution.py:137
  1244.6 98.9 %collective-permute-start.50 = (bf16[2,128,2560]{2,1,0:T(8,128)(2,1)}, bf16[2,128,2560]{2,1,0:T(8,128)(2,1)}, u32[]{:S(2)}, u32[]{:S(2)}) collective-permute-start(bf16[2,128,2560]{2,1,0:T(8,128)(2,1)} %collective-permute-done.49.refs_2_), channel_id=1, source_target_pairs={{8,12},{9,13},{10,14},{11,15},{24,28},{25,29},{26,30},{27,31}} | collective-permute-start | bytes 3932168 | tf_op jit(solution)/shard_map/ppermute | solution.py:136
  1246.4 97.1 %collective-permute-start.53 = (bf16[2,128,2560]{2,1,0:T(8,128)(2,1)}, bf16[2,128,2560]{2,1,0:T(8,128)(2,1)}, u32[]{:S(2)}, u32[]{:S(2)}) collective-permute-start(bf16[2,128,2560]{2,1,0:T(8,128)(2,1)} %collective-permute-done.52.refs_5_), channel_id=1, source_target_pairs={{4,0},{5,1},{6,2},{7,3},{20,16},{21,17},{22,18},{23,19}} | collective-permute-start | bytes 3932168 | tf_op jit(solution)/shard_map/ppermute | solution.py:137
  1454.7 243.8 %collective-permute-start.93 = (bf16[2,128,2560]{2,1,0:T(8,128)(2,1)}, bf16[2,128,2560]{2,1,0:T(8,128)(2,1)}, u32[]{:S(2)}, u32[]{:S(2)}) collective-permute-start(bf16[2,128,2560]{2,1,0:T(8,128)(2,1)} %get-tuple-element.273), channel_id=1, source_target_pairs={{0,4},{12,8},{1,5},{13,9},{2,6},{14,10},{3,7},{15,11},{16,20},{28,... | collective-permute-start | bytes 3932168 | tf_op jit(solution)/shard_map/ppermute | solution.py:142
  1535.0 159.2 %collective-permute-start.78 = (bf16[2,128,2560]{2,1,0:T(8,128)(2,1)}, bf16[2,128,2560]{2,1,0:T(8,128)(2,1)}, u32[]{:S(2)}, u32[]{:S(2)}) collective-permute-start(bf16[2,128,2560]{2,1,0:T(8,128)(2,1)} %get-tuple-element.255), channel_id=1, source_target_pairs={{0,4},{12,8},{1,5},{13,9},{2,6},{14,10},{3,7},{15,11},{16,20},{28,... | collective-permute-start | bytes 3932168 | tf_op jit(solution)/shard_map/ppermute | solution.py:142
  1615.0 86.2 %collective-permute-start.66 = (bf16[2,128,2560]{2,1,0:T(8,128)(2,1)}, bf16[2,128,2560]{2,1,0:T(8,128)(2,1)}, u32[]{:S(2)}, u32[]{:S(2)}) collective-permute-start(bf16[2,128,2560]{2,1,0:T(8,128)(2,1)} %get-tuple-element.237), channel_id=1, source_target_pairs={{0,4},{12,8},{1,5},{13,9},{2,6},{14,10},{3,7},{15,11},{16,20},{28,... | collective-permute-start | bytes 3932168 | tf_op jit(solution)/shard_map/ppermute | solution.py:142
  1728.3 79.4 %collective-permute-start.94 = (bf16[2,128,2560]{2,1,0:T(8,128)(2,1)S(1)}, bf16[2,128,2560]{2,1,0:T(8,128)(2,1)S(1)}, u32[]{:S(2)}, u32[]{:S(2)}) collective-permute-start(bf16[2,128,2560]{2,1,0:T(8,128)(2,1)S(1)} %add.352), channel_id=1, source_target_pairs={{0,4},{4,8},{1,5},{5,9},{2,6},{6,10},{3,7},{7,11},{16,20},{20,24},... | collective-permute-start | bytes 3932168 | tf_op jit(solution)/shard_map/ppermute | solution.py:144
  1753.0 82.8 %collective-permute-start.55 = (bf16[2,128,2560]{2,1,0:T(8,128)(2,1)S(1)}, bf16[2,128,2560]{2,1,0:T(8,128)(2,1)S(1)}, u32[]{:S(2)}, u32[]{:S(2)}) collective-permute-start(bf16[2,128,2560]{2,1,0:T(8,128)(2,1)S(1)} %add.325), channel_id=1, source_target_pairs={{0,4},{4,8},{1,5},{5,9},{2,6},{6,10},{3,7},{7,11},{16,20},{20,24},... | collective-permute-start | bytes 3932168 | tf_op jit(solution)/shard_map/ppermute | solution.py:144
  1758.1 79.3 %collective-permute-start.82 = (bf16[2,128,2560]{2,1,0:T(8,128)(2,1)S(1)}, bf16[2,128,2560]{2,1,0:T(8,128)(2,1)S(1)}, u32[]{:S(2)}, u32[]{:S(2)}) collective-permute-start(bf16[2,128,2560]{2,1,0:T(8,128)(2,1)S(1)} %add.344), channel_id=1, source_target_pairs={{12,8},{8,4},{4,0},{13,9},{9,5},{5,1},{14,10},{10,6},{6,2},{15,11}... | collective-permute-start | bytes 3932168 | tf_op jit(solution)/shard_map/ppermute | solution.py:148
  1779.6 84.3 %collective-permute-start.80 = (bf16[2,128,2560]{2,1,0:T(8,128)(2,1)S(1)}, bf16[2,128,2560]{2,1,0:T(8,128)(2,1)S(1)}, u32[]{:S(2)}, u32[]{:S(2)}) collective-permute-start(bf16[2,128,2560]{2,1,0:T(8,128)(2,1)S(1)} %add.342), channel_id=1, source_target_pairs={{0,4},{4,8},{8,12},{1,5},{5,9},{9,13},{2,6},{6,10},{10,14},{3,7},{... | collective-permute-start | bytes 3932168 | tf_op jit(solution)/shard_map/ppermute | solution.py:147
  1809.0 81.3 %collective-permute-start.68 = (bf16[2,128,2560]{2,1,0:T(8,128)(2,1)S(1)}, bf16[2,128,2560]{2,1,0:T(8,128)(2,1)S(1)}, u32[]{:S(2)}, u32[]{:S(2)}) collective-permute-start(bf16[2,128,2560]{2,1,0:T(8,128)(2,1)S(1)} %add.334), channel_id=1, source_target_pairs={{0,4},{4,8},{8,12},{1,5},{5,9},{9,13},{2,6},{6,10},{10,14},{3,7},{... | collective-permute-start | bytes 3932168 | tf_op jit(solution)/shard_map/ppermute | solution.py:147
  1835.8 100.3 %collective-permute-start.46 = (bf16[8,128,640]{2,1,0:T(8,128)(2,1)S(1)}, bf16[8,128,640]{2,1,0:T(8,128)(2,1)S(1)}, u32[]{:S(2)}, u32[]{:S(2)}) collective-permute-start(bf16[8,128,640]{2,1,0:T(8,128)(2,1)S(1)} %pad_maximum_fusion.2), channel_id=1, source_target_pairs={{3,2},{7,6},{11,10},{15,14},{19,18},{23,22},{27,26},{31,30}} | collective-permute-start | bytes 3932168 | tf_op jit(solution)/shard_map/ppermute | solution.py:204
  1869.2 68.3 %collective-permute-start.45 = (bf16[8,128,640]{2,1,0:T(8,128)(2,1)S(1)}, bf16[8,128,640]{2,1,0:T(8,128)(2,1)S(1)}, u32[]{:S(2)}, u32[]{:S(2)}) collective-permute-start(bf16[8,128,640]{2,1,0:T(8,128)(2,1)S(1)} %pad_maximum_fusion.1), channel_id=1, source_target_pairs={{3,1},{7,5},{11,9},{15,13},{19,17},{23,21},{27,25},{31,29}} | collective-permute-start | bytes 3932168 | tf_op jit(solution)/shard_map/ppermute | solution.py:204
  (196 other events, 7295.3 us)
